TPU v7x, 128 devices: a whole 4x4x4 slice. The times are simulated.
128 devices in a mesh: grp: 4 (over y), dom: 32 (over z, x, core).
Axes of the slice: x: 4, y: 4, z: 4, core: 2. Of those that a mesh axis runs over, the one named last changes fastest.
Arguments:
- table: float32 [524288, 256], P(('grp', 'dom')), may hold values from -6 to 6
- accum: float32 [524288], P(('grp', 'dom')), may hold values from 1e-07 to 0.0001
- w_self1: bfloat16 [256, 1024], replicated, may hold values from -0.375 to 0.375
- w_nbr1: bfloat16 [256, 1024], replicated, may hold values from -0.375 to 0.375
- w_self2: bfloat16 [1024, 1024], replicated, may hold values from -0.1875 to 0.1875
- w_nbr2: bfloat16 [1024, 1024], replicated, may hold values from -0.1875 to 0.1875
- fetch_owner: int32 [131072, 1], P(('grp', 'dom')), may hold values from 0 to 127; in each aligned block of 1024 rows (0 to 1023, 1024 to 2047, ...) at most 16 rows name the same one
- fetch_row: int32 [131072], P(('grp', 'dom')), may hold values from 0 to 4095
- self_slot: int32 [131072], P(('grp', 'dom')), may hold values from 0 to 1023
- nbr_one: int32 [131072, 8], P(('grp', 'dom')), may hold values from 0 to 1023
- nbr_two: int32 [131072, 8], P(('grp', 'dom')), may hold values from 0 to 1151
- cotangent: float32 [131072, 1024], P(('grp', 'dom')), may hold values from -0.06 to 0.06
Outputs:
- embedded: bfloat16 [131072, 1024], P(('grp', 'dom'))
- new_table: float32 [524288, 256], P(('grp', 'dom'))
- new_accum: float32 [524288], P(('grp', 'dom'))
- grad_self1: bfloat16 [256, 1024], replicated
- grad_nbr1: bfloat16 [256, 1024], replicated
- grad_self2: bfloat16 [1024, 1024], replicated
- grad_nbr2: bfloat16 [1024, 1024], replicated
Inputs may be any that keep to these rules, and one draw needn't show every extreme that they name: `fetch_owner`: among the 1024 requests of one partition at most 16 name the same owner, and in some partition one owner is named exactly 16 times.
All inputs are finite; a program needn't handle non-finite values.
Results may differ from a plain program's by a relative error of at most 0.0045.
The roundings to bfloat16 on the way count: a program that leaves them out, or rounds other values in their place, can miss the bound.
Values may be sent and summed in bfloat16 or wider, within the bound.
No kernel may reach another device: no remote copies, remote signals or barrier semaphores. Data moves between devices by JAX's collectives and lax.ppermute only.
A program may use at most 128 MiB of HBM per device.

v0:
```python
import jax
import jax.numpy as jnp
from jax import lax
from jax.experimental import pallas as pl
from jax.experimental.pallas import tpu as pltpu
from jax.sharding import PartitionSpec as P


BORDER = 64
AXES = ("grp", "dom")
epsilon = 1e-06
learning_rate = 0.1
BF = jnp.bfloat16
F32 = jnp.float32
I32 = jnp.int32
I16 = jnp.int16
MIB = 1024 * 1024


def iota(shape, dim):
    return lax.broadcasted_iota(I32, shape, dim)


def nn(a, b):
    return lax.dot_general(a, b, (((1,), (0,)), ((), ())), preferred_element_type=F32)


def nt(a, b):
    return lax.dot_general(a, b, (((1,), (1,)), ((), ())), preferred_element_type=F32)


def tn(a, b):
    return lax.dot_general(a, b, (((0,), (0,)), ((), ())), preferred_element_type=F32)


def hot(mask):
    return jnp.where(mask, 1.0, 0.0).astype(BF)


def hot_lanes(col, width):
    lanes = col.shape[1]
    index = iota(col.shape, 1).astype(I16)
    parts = []
    for at in range(0, width, lanes):
        hit = col == index + jnp.full(col.shape, at, I16)
        parts.append(jnp.where(hit, jnp.ones(col.shape, BF), jnp.zeros(col.shape, BF)))
    return jnp.concatenate(parts, axis=1)


def hot_rows(row, rows, first):
    shape = (rows, row.shape[1])
    index = iota(shape, 0).astype(I16)
    wanted = jnp.broadcast_to(row - first, shape).astype(I16)
    return jnp.where(index == wanted, jnp.ones(shape, BF), jnp.zeros(shape, BF))


def to_lanes(row):
    return jnp.broadcast_to(row, (128, row.shape[1])).T.astype(I16)


def logistic(v):
    return 1.0 / (1.0 + jnp.exp(-v))


def params(mib, *semantics):
    return pltpu.CompilerParams(
        dimension_semantics=semantics if semantics else None, vmem_limit_bytes=mib * MIB
    )


def in_hbm(x):
    return pltpu.with_memory_space_constraint(x, pltpu.HBM)


def cost(flops):
    return pl.CostEstimate(flops=flops, bytes_accessed=4 << 20, transcendentals=0)


def prep_kernel(owner_ref, row_ref, pos_ref, wanted_ref):
    count = owner_ref.shape[1]
    devices, cap = wanted_ref.shape
    owner = owner_ref[...]
    row = row_ref[...]
    owner_hot = hot(iota((devices, count), 0) == owner)
    earlier = hot(iota((count, count), 0) < iota((count, count), 1))
    before = nn(owner_hot, earlier)
    rank = jnp.sum(before * owner_hot.astype(F32), axis=0, keepdims=True).astype(I32)
    pos_ref[...] = owner * cap + rank
    at_rank = iota((cap, count), 0) == rank
    high = jnp.where(at_rank, (row >> 6).astype(F32), 0.0).astype(BF)
    low = jnp.where(at_rank, (row & 63).astype(F32), 0.0).astype(BF)
    wanted_ref[...] = (nt(owner_hot, high) * 64.0 + nt(owner_hot, low)).astype(I32)


def prep(owner, row, devices, cap):
    count = owner.shape[1]
    return pl.pallas_call(
        prep_kernel,
        out_shape=(
            jax.ShapeDtypeStruct((1, count), I32),
            jax.ShapeDtypeStruct((devices, cap), I32),
        ),
        compiler_params=params(8),
        name="prep",
    )(owner, row)


def counts_kernel(shift, width, nbr_ref, *out_refs):
    fanout, lanes = nbr_ref.shape
    base = 0
    lists = []
    for k in range(fanout):
        row = nbr_ref[k : k + 1, :]
        if shift:
            row = row - shift
            row = jnp.where(row < 0, row + width, row)
        lists.append(jnp.broadcast_to(row, (16, lanes)).astype(I16))
    index = iota((16, lanes), 0).astype(I16)
    unit = jnp.full((16, lanes), 1.0 / fanout, BF)
    none = jnp.zeros((16, lanes), BF)
    for adj_t_ref, adj_ref in zip(out_refs[::2], out_refs[1::2]):
        for first in range(0, adj_t_ref.shape[0], 128):
            rows = []
            for r in range(first, first + 128, 16):
                at = index + jnp.full((16, lanes), base + r, I16)
                acc = none
                for k in range(fanout):
                    acc = acc + jnp.where(lists[k] == at, unit, none)
                rows.append(acc)
            block = jnp.concatenate(rows, axis=0)
            adj_t_ref[first : first + 128, :] = block
            adj_ref[:, first : first + 128] = block.T
        base += adj_t_ref.shape[0]


def counts(nbr_t, widths, shift):
    fanout, nodes = nbr_t.shape
    block = 128
    specs, shapes = [], []
    for width in widths:
        specs += [
            pl.BlockSpec((width, block), lambda i: (0, i)),
            pl.BlockSpec((block, width), lambda i: (i, 0)),
        ]
        shapes += [pltpu.HBM((width, nodes), BF), pltpu.HBM((nodes, width), BF)]
    return pl.pallas_call(
        lambda *refs: counts_kernel(shift, sum(widths), *refs),
        grid=(nodes // block,),
        in_specs=[pl.BlockSpec((fanout, block), lambda i: (0, i))],
        out_specs=specs,
        out_shape=shapes,
        compiler_params=params(8, "arbitrary"),
        cost_estimate=cost(4 << 30),
    )(nbr_t)


def pick_kernel(inc_ref, table_ref, out_ref, col_ref, acc_ref, turn_ref):
    i = pl.program_id(0)
    peers, cap = inc_ref.shape
    rows, width = table_ref.shape

    @pl.when(i == 0)
    def _():
        for c in range(cap):
            col_ref[c * peers : (c + 1) * peers, :] = jnp.broadcast_to(
                inc_ref[:, c : c + 1], (peers, 128)
            ).astype(I16)

    def step(j, carry):
        first = pl.multiple_of(j * 256, 256)
        chunk = table_ref[pl.ds(first, 256), :].astype(BF)
        base = (jnp.zeros(col_ref.shape, I32) + (i * rows + first)).astype(I16)
        part = nn(hot_lanes(col_ref[...] - base, 256), chunk)
        fresh = jnp.logical_and(i == 0, j == 0)

        @pl.when(fresh)
        def _():
            acc_ref[...] = part

        @pl.when(jnp.logical_not(fresh))
        def _():
            acc_ref[...] += part

        return carry

    lax.fori_loop(0, rows // 256, step, 0)

    @pl.when(i == pl.num_programs(0) - 1)
    def _():
        for c in range(cap):
            for h in range(width // 128):
                turn_ref.at[h][pl.ds(c, peers, stride=cap), :] = acc_ref[
                    c * peers : (c + 1) * peers, h * 128 : (h + 1) * 128
                ]
        for h in range(width // 128):
            out_ref[:, h * 128 : (h + 1) * 128] = turn_ref[h].astype(BF)


def pick(incoming, table):
    devices, cap = incoming.shape
    rows, width = table.shape
    slots = devices * cap
    block = 1024
    return pl.pallas_call(
        pick_kernel,
        grid=(rows // block,),
        in_specs=[
            pl.BlockSpec((devices, cap), lambda i: (0, 0)),
            pl.BlockSpec((block, width), lambda i: (i, 0)),
        ],
        out_specs=pl.BlockSpec((slots, width), lambda i: (0, 0)),
        out_shape=pltpu.HBM((slots, width), BF),
        scratch_shapes=[
            pltpu.VMEM((slots, 128), I16),
            pltpu.VMEM((slots, width), F32),
            pltpu.VMEM((width // 128, slots, 128), F32),
        ],
        compiler_params=params(24, "arbitrary"),
        name="pick",
    )(incoming, in_hbm(table))


def layer_one_kernel(
    pos_ref, slot_ref, replies_ref, adj_ref, ws_ref, wn_ref,
    selfs_ref, pooled_ref, before_ref, hidden_ref, fetched_ref,
):
    i = pl.program_id(0)
    _, fetch = adj_ref.shape
    slots = replies_ref.shape[0]

    @pl.when(i == 0)
    def _():
        for at in range(0, fetch, 512):
            place = hot_lanes(to_lanes(pos_ref[:, at : at + 512]), slots)
            fetched_ref[at : at + 512, :] = nn(place, replies_ref[...]).astype(BF)

    @pl.when(i > 0)
    def _():
        self_hot = hot_lanes(to_lanes(slot_ref[...]), fetch)
        selfs = nn(self_hot, fetched_ref[...]).astype(BF)
        pooled = nn(adj_ref[...], fetched_ref[...]).astype(BF)
        selfs_ref[...] = selfs
        pooled_ref[...] = pooled
        before = nn(selfs, ws_ref[...]) + nn(pooled, wn_ref[...])
        before_ref[...] = before
        hidden_ref[...] = (before * logistic(before)).astype(BF)


def layer_one(pos, slot, replies, adj, w_self, w_nbr):
    nodes, fetch = adj.shape
    slots = replies.shape[0]
    emb, hid = w_self.shape
    block = 512
    late = lambda i: (jnp.maximum(i - 1, 0), 0)
    whole = lambda i: (0, 0)
    return pl.pallas_call(
        layer_one_kernel,
        grid=(1 + nodes // block,),
        in_specs=[
            pl.BlockSpec((1, fetch), whole),
            pl.BlockSpec((1, block), lambda i: (0, jnp.maximum(i - 1, 0))),
            pl.BlockSpec((slots, emb), whole),
            pl.BlockSpec((block, fetch), late),
            pl.BlockSpec((emb, hid), whole),
            pl.BlockSpec((emb, hid), whole),
        ],
        out_specs=[
            pl.BlockSpec((block, emb), late),
            pl.BlockSpec((block, emb), late),
            pl.BlockSpec((block, hid), late),
            pl.BlockSpec((block, hid), late),
        ],
        out_shape=(
            pltpu.HBM((nodes, emb), BF),
            pltpu.HBM((nodes, emb), BF),
            pltpu.HBM((nodes, hid), F32),
            jax.ShapeDtypeStruct((nodes, hid), BF),
        ),
        scratch_shapes=[pltpu.VMEM((fetch, emb), BF)],
        compiler_params=params(28, "arbitrary"),
        name="layer_one",
    )(pos, slot, in_hbm(replies), in_hbm(adj), in_hbm(w_self), in_hbm(w_nbr))


def layer_two_kernel(
    own_ref, pool_ref, edge_ref, edge_t_ref, after_ref, before_in_ref, wn_ref, up_ref,
    emb_ref, pooled_ref, grad_ref, gpool_ref, gedge_ref,
):
    i = pl.program_id(0)
    halo = jnp.concatenate([after_ref[...], before_in_ref[...]], axis=0)
    pooled = (pool_ref[...] + nn(edge_ref[...], halo)).astype(BF)
    pooled_ref[...] = pooled
    before = own_ref[...] + nn(pooled, wn_ref[...])
    gate = logistic(before)
    lifted = before * gate
    scale = lax.rsqrt(jnp.mean(lifted * lifted, axis=1, keepdims=True) + epsilon)
    normed = lifted * scale
    emb_ref[...] = normed.astype(BF)
    up = up_ref[...]
    grad_lifted = scale * (up - normed * jnp.mean(up * normed, axis=1, keepdims=True))
    grad = (grad_lifted * (gate + lifted * (1.0 - gate))).astype(BF)
    grad_ref[...] = grad
    gpool = nt(grad, wn_ref[...]).astype(BF)
    gpool_ref[...] = gpool
    part = nn(edge_t_ref[...], gpool)

    @pl.when(i == 0)
    def _():
        gedge_ref[...] = part

    @pl.when(i > 0)
    def _():
        gedge_ref[...] += part


def layer_two(own, pool, edge, edge_t, after, before, w_nbr, upstream):
    nodes, hid = own.shape
    block = 256
    rows = lambda i: (i, 0)
    whole = lambda i: (0, 0)
    return pl.pallas_call(
        layer_two_kernel,
        grid=(nodes // block,),
        in_specs=[
            pl.BlockSpec((block, hid), rows),
            pl.BlockSpec((block, hid), rows),
            pl.BlockSpec((block, 2 * BORDER), rows),
            pl.BlockSpec((2 * BORDER, block), lambda i: (0, i)),
            pl.BlockSpec((BORDER, hid), whole),
            pl.BlockSpec((BORDER, hid), whole),
            pl.BlockSpec((hid, hid), whole),
            pl.BlockSpec((block, hid), rows),
        ],
        out_specs=[
            pl.BlockSpec((block, hid), rows),
            pl.BlockSpec((block, hid), rows),
            pl.BlockSpec((block, hid), rows),
            pl.BlockSpec((block, hid), rows),
            pl.BlockSpec((2 * BORDER, hid), whole),
        ],
        out_shape=(
            jax.ShapeDtypeStruct((nodes, hid), BF),
            jax.ShapeDtypeStruct((nodes, hid), BF),
            jax.ShapeDtypeStruct((nodes, hid), BF),
            jax.ShapeDtypeStruct((nodes, hid), BF),
            jax.ShapeDtypeStruct((2 * BORDER, hid), F32),
        ),
        compiler_params=params(28, "arbitrary"),
        name="layer_two",
    )(own, pool, edge, edge_t, after, before, w_nbr, upstream)


def back_one_kernel(
    gh_ref, first_ref, last_ref, before_ref, slot_ref, adj_t_ref, ws_ref, wn_ref, pos_ref,
    grad_ref, out_ref, gh_scr, acc_ref,
):
    i = pl.program_id(0)
    last = pl.num_programs(0) - 1
    block = gh_ref.shape[0]
    fetch = acc_ref.shape[0]
    gh_scr[...] = gh_ref[...]

    @pl.when(i == 0)
    def _():
        gh_scr[0:BORDER, :] += first_ref[...]

    @pl.when(i == last)
    def _():
        gh_scr[block - BORDER : block, :] += last_ref[...]

    before = before_ref[...]
    gate = logistic(before)
    grad = (gh_scr[...] * (gate + before * gate * (1.0 - gate))).astype(BF)
    grad_ref[...] = grad
    gself = nt(grad, ws_ref[...])
    high = gself.astype(BF)
    low = (gself - high.astype(F32)).astype(BF)
    gpool = nt(grad, wn_ref[...]).astype(BF)
    self_t = hot_rows(slot_ref[...], fetch, 0)
    part = nn(self_t, high) + nn(self_t, low) + nn(adj_t_ref[...], gpool)

    @pl.when(i == 0)
    def _():
        acc_ref[...] = part

    @pl.when(i > 0)
    def _():
        acc_ref[...] += part

    @pl.when(i == last)
    def _():
        total = acc_ref[...].astype(BF)
        pos = pos_ref[...]
        slots = out_ref.shape[0]
        for at in range(0, slots, 256):
            place_t = hot_rows(pos, 256, at)
            out_ref[at : at + 256, :] = nn(place_t, total).astype(BF)


def back_one(gh, first, last, before, slot, adj_t, w_self, w_nbr, pos, slots):
    nodes, hid = gh.shape
    emb = w_self.shape[0]
    fetch = adj_t.shape[0]
    block = 256
    rows = lambda i: (i, 0)
    cols = lambda i: (0, i)
    whole = lambda i: (0, 0)
    return pl.pallas_call(
        back_one_kernel,
        grid=(nodes // block,),
        in_specs=[
            pl.BlockSpec((block, hid), rows),
            pl.BlockSpec((BORDER, hid), whole),
            pl.BlockSpec((BORDER, hid), whole),
            pl.BlockSpec((block, hid), rows),
            pl.BlockSpec((1, block), cols),
            pl.BlockSpec((fetch, block), cols),
            pl.BlockSpec((emb, hid), whole),
            pl.BlockSpec((emb, hid), whole),
            pl.BlockSpec((1, fetch), whole),
        ],
        out_specs=[
            pl.BlockSpec((block, hid), rows),
            pl.BlockSpec((slots, emb), whole),
        ],
        out_shape=(
            pltpu.HBM((nodes, hid), BF),
            pltpu.HBM((slots, emb), BF),
        ),
        scratch_shapes=[pltpu.VMEM((block, hid), F32), pltpu.VMEM((fetch, emb), F32)],
        compiler_params=params(24, "arbitrary"),
        name="back_one",
    )(gh, first, last, before, slot, adj_t, w_self, w_nbr, pos)


def update_kernel(
    inc_ref, got_ref, table_ref, accum_ref, new_table_ref, new_accum_ref, returned_ref
):
    i = pl.program_id(0)
    block, width = table_ref.shape
    slots = returned_ref.shape[0]
    peers = got_ref.shape[0]

    @pl.when(i == 0)
    def _():
        returned_ref[...] = got_ref[:, : slots // peers, :].reshape(slots, width)

    inc = inc_ref[...]
    step = 512
    grads = jnp.zeros((block, width), F32)
    for at in range(0, slots, step):
        rows_hot = hot_rows(inc[:, at : at + step], block, i * block)
        grads = grads + nn(rows_hot, returned_ref[at : at + step, :])
    square = jnp.mean(grads * grads, axis=1, keepdims=True)
    accum = accum_ref[0]
    new_accum_ref[0] = accum + jnp.broadcast_to(square, (block, 128)).T[0:1, :]
    total = jnp.broadcast_to(accum, (128, block)).T + square
    factor = learning_rate / (jnp.sqrt(total) + epsilon)
    for at in range(0, width, 128):
        new_table_ref[:, at : at + 128] = (
            table_ref[:, at : at + 128] - grads[:, at : at + 128] * factor
        )


def update(inc_row, got, table, accum):
    rows, width = table.shape
    slots = inc_row.shape[1]
    block = 512
    shaped = accum.reshape(rows // block, 1, block)
    new_table, new_accum = pl.pallas_call(
        update_kernel,
        grid=(rows // block,),
        in_specs=[
            pl.BlockSpec((1, slots), lambda i: (0, 0)),
            pl.BlockSpec(got.shape, lambda i: (0, 0, 0)),
            pl.BlockSpec((block, width), lambda i: (i, 0)),
            pl.BlockSpec((1, 1, block), lambda i: (i, 0, 0)),
        ],
        out_specs=[
            pl.BlockSpec((block, width), lambda i: (i, 0)),
            pl.BlockSpec((1, 1, block), lambda i: (i, 0, 0)),
        ],
        out_shape=(
            jax.ShapeDtypeStruct((rows, width), F32),
            jax.ShapeDtypeStruct(shaped.shape, F32),
        ),
        scratch_shapes=[pltpu.VMEM((slots, width), BF)],
        compiler_params=params(16, "arbitrary"),
        cost_estimate=cost(4 << 30),
        name="update",
    )(inc_row, in_hbm(got), in_hbm(table), shaped)
    return new_table, new_accum.reshape(rows)


def chip_sums(parts_ref, core):
    total = parts_ref[core].astype(F32)
    for at in range(core + 2, parts_ref.shape[0], 2):
        total = total + parts_ref[at].astype(F32)
    return total.astype(BF)


def two_sum_kernel(parts_ref, out_ref):
    for core in range(2):
        out_ref[core] = chip_sums(parts_ref, core)


def two_sum(parts):
    peers, rows, width = parts.shape
    lanes = 512
    return pl.pallas_call(
        two_sum_kernel,
        grid=(width // lanes,),
        in_specs=[pl.BlockSpec((peers, rows, lanes), lambda i: (0, 0, i))],
        out_specs=pl.BlockSpec((2, rows, lanes), lambda i: (0, 0, i)),
        out_shape=jax.ShapeDtypeStruct((2, rows, width), BF),
        compiler_params=params(8, "arbitrary"),
        cost_estimate=cost(1 << 30),
        name="two_sum",
    )(in_hbm(parts))


def spread_kernel(two_ref, got_ref, out_ref):
    i = pl.program_id(0)
    peers = out_ref.shape[0]
    last = pl.num_programs(0) - 1

    @pl.when(i < last)
    def _():
        for core in range(2):
            for at in range(core, peers, 2):
                out_ref[at] = two_ref[core]

    @pl.when(i == last)
    def _():
        for core in range(2):
            total = chip_sums(got_ref, core)
            for at in range(core, peers, 2):
                out_ref[at] = total


def spread(two, got):
    rows, width = two.shape[1:]
    peers, held, lanes = got.shape
    steps = width // lanes
    return pl.pallas_call(
        spread_kernel,
        grid=(steps + 1,),
        in_specs=[
            pl.BlockSpec((2, rows, lanes), lambda i: (0, 0, jnp.minimum(i, steps - 1))),
            pl.BlockSpec((peers, rows, lanes), lambda i: (0, held // rows - 1, 0)),
        ],
        out_specs=pl.BlockSpec((peers, rows, lanes), lambda i: (0, 0, i)),
        out_shape=pltpu.HBM((peers, rows, width + lanes), BF),
        compiler_params=params(8, "arbitrary"),
        name="spread",
    )(two, in_hbm(got))


def exchange(x):
    return lax.all_to_all(x, AXES, 0, 0, tiled=True)


def core_pairs():
    return [(i, i ^ 1) for i in range(lax.axis_size("dom"))]


def chip_grads(left, right, grad):
    first_core = lax.axis_index("dom") % 2 == 0
    theirs = tn(jnp.where(first_core, right, left), grad).astype(BF)
    arrived = lax.ppermute(theirs, "dom", core_pairs())
    ours = tn(jnp.where(first_core, left, right), grad)
    return (ours + arrived.astype(F32)).astype(BF)


def local(
    table, accum, w_self1, w_nbr1, w_self2, w_nbr2,
    fetch_owner, fetch_row, self_slot, nbr_one, nbr_two, cotangent,
):
    devices = lax.axis_size("grp") * lax.axis_size("dom")
    count = fetch_row.shape[0]
    emb = table.shape[1]
    nodes = self_slot.shape[0]
    cap = max(2, 2 * count // devices)
    slots = devices * cap
    ring_up = [(i, (i + 1) % devices) for i in range(devices)]
    ring_down = [(j, i) for i, j in ring_up]
    slot_row = self_slot.reshape(1, nodes)

    pos, wanted = prep(fetch_owner.reshape(1, count), fetch_row.reshape(1, count), devices, cap)
    incoming = exchange(wanted)
    mid_t, mid, edge_t, edge = counts(nbr_two.T, (nodes, 2 * BORDER), BORDER)
    found = pick(incoming, table)
    replies = exchange(found.reshape(devices, cap, emb))
    adj_t, adj = counts(nbr_one.T, (count,), 0)
    inc_row = incoming.reshape(1, slots)

    selfs, pooled_one, before_one, hidden = layer_one(
        pos, slot_row, replies.reshape(slots, emb), adj, w_self1, w_nbr1
    )
    before = lax.ppermute(hidden[nodes - BORDER :], AXES, ring_up)
    after = lax.ppermute(hidden[:BORDER], AXES, ring_down)
    own = nn(hidden, w_self2)
    pool = nn(mid, hidden)
    embedded, pooled_two, grad_two, grad_pool, grad_edge = layer_two(
        own, pool, edge, edge_t, after, before, w_nbr2, cotangent
    )
    to_first = lax.ppermute(grad_edge[:BORDER], AXES, ring_up)
    to_last = lax.ppermute(grad_edge[BORDER:], AXES, ring_down)
    chip_two = chip_grads(hidden, pooled_two, grad_two)
    hid = chip_two.shape[1]
    parts_two = exchange(chip_two.reshape(devices, -1, hid))
    grad_hidden = nt(grad_two, w_self2) + nn(mid_t, grad_pool)
    grad_one, grad_slots = back_one(
        grad_hidden, to_first, to_last, before_one, slot_row, adj_t, w_self1, w_nbr1, pos, slots
    )
    chip_one = chip_grads(selfs, pooled_one, grad_one)
    down, across = chip_one.shape[0] // 8, chip_one.shape[1] // emb
    tiles = chip_one.reshape(down, 8, across, emb).transpose(2, 0, 1, 3)
    sent = jnp.concatenate(
        [grad_slots.reshape(devices, cap, emb), tiles.reshape(devices, 8, emb)], axis=1
    )
    got = exchange(sent)
    mine = exchange(spread(two_sum(parts_two), got))
    new_table, new_accum = update(inc_row, got, table, accum)
    other = lax.ppermute(mine, "dom", core_pairs())
    first_core = lax.axis_index("dom") % 2 == 0

    def of_one(x):
        x = x[:, :, hid:].reshape(across, down, 8, emb).transpose(1, 2, 0, 3)
        return x.reshape(chip_one.shape)

    def of_two(x):
        return x[:, :, :hid].reshape(chip_two.shape)

    grads = []
    for of in (of_one, of_two):
        grads.append(of(jnp.where(first_core, mine, other)))
        grads.append(of(jnp.where(first_core, other, mine)))
    return (embedded, new_table, new_accum) + tuple(grads)


def solution(mesh):
    rows = P(AXES, None)
    flat = P(AXES)
    in_specs = (rows, flat, P(), P(), P(), P(), rows, flat, flat, rows, rows, rows)
    out_specs = (rows, rows, flat, P(), P(), P(), P())
    return jax.shard_map(
        local, mesh=mesh, in_specs=in_specs, out_specs=out_specs, check_vma=False
    )
```

profile of v0, /device:TPU:1, one launch (start us, length us, event | category | flops | bytes accessed | tf_op | source)
XLA Modules:
  0.0 240.9 jit_solution(485550455489785813)
XLA Ops:
  0.7 0.8 copy-done.11
  1.5 0.7 copy-done.12
  2.2 0.7 prep.1
  2.8 20.8 %all_to_all.31 = s32[128,1,16]{2,1,0:T(1,128)S(1)} all-to-all(s32[128,1,16]{2,1,0:T(1,128)S(1)} %bitcast.49), channel_id=1, replica_groups=mesh['grp'=4,'dom'=32] {'grp','dom'}, dimensions={0} | all-to-all | bytes 16384 | tf_op jit(solution)/shard_map/all_to_all | solution.py:560
  23.7 14.2 %pick.1 = bf16[2048,256]{1,0:T(8,128)(2,1)} custom-call(s32[128,16]{1,0:T(8,128)S(1)} %bitcast.48, f32[4096,256]{1,0:T(8,128)} %table_ref.3), custom_call_target="tpu_custom_call" | custom-call | tf_op jit(solution)/shard_map/pick/pallas_call | solution.py:204
  37.9 4.6 %all-to-all-start.1 = ((bf16[128,16,256]{2,1,0:T(8,128)(2,1)}), bf16[128,16,256]{2,1,0:T(8,128)(2,1)S(1)}, u32[]{:S(2)}, u32[]{:S(2)}) async-start(bf16[128,16,256]{2,1,0:T(8,128)(2,1)} %bitcast.58), calls=%async_computation.1 | async-start | bytes 2097152 | tf_op jit(solution)/shard_map/all_to_all | solution.py:560
  42.5 4.5 %shard_map.171 = (bf16[1024,1024]{1,0:T(8,128)(2,1)}, bf16[1024,1024]{1,0:T(8,128)(2,1)}) custom-call(s32[8,1024]{1,0:T(8,128)S(1)} %bitcast.54), custom_call_target="tpu_custom_call" | custom-call | flops 4294967296 | bytes 4194304 | tf_op jit(solution)/shard_map/pallas_call | solution.py:146
  47.0 4.7 %shard_map.172 = (bf16[1024,1024]{1,0:T(8,128)(2,1)}, bf16[1024,1024]{1,0:T(8,128)(2,1)}, bf16[128,1024]{1,0:T(8,128)(2,1)}, bf16[1024,128]{1,0:T(8,128)(2,1)}) custom-call(s32[8,1024]{1,0:T(8,128)S(1)} %bitcast.55), custom_call_target="tpu_custom_call" | custom-call | flops 4294967296 | bytes 4194304 | tf_op jit(solution)/shard_map/pallas_call | solution.py:146
  51.7 10.0 %all-to-all-done.1 = bf16[128,16,256]{2,1,0:T(8,128)(2,1)S(1)} async-done(((bf16[128,16,256]{2,1,0:T(8,128)(2,1)}), bf16[128,16,256]{2,1,0:T(8,128)(2,1)S(1)}, u32[]{:S(2)}, u32[]{:S(2)}) %all-to-all-start.1) | async-done | bytes 1048608 | tf_op jit(solution)/shard_map/all_to_all | solution.py:560
  61.7 1.0 copy-done.21
  62.7 7.8 %layer_one.1 = (bf16[1024,256]{1,0:T(8,128)(2,1)}, bf16[1024,256]{1,0:T(8,128)(2,1)}, f32[1024,1024]{1,0:T(8,128)}, bf16[1024,1024]{1,0:T(8,128)(2,1)S(1)}) custom-call(s32[1,1024]{1,0:T(1,128)S(1)} %get-tuple-element.28.pos_ref, s32[1,1024]{1,0:T(1,128)S(1)} %bitcast.50, bf16[2048,256]{1,0:T(8,128)(2,1)} %bitcast.57, ...), custom_call_target="tpu_custom_call" | custom-call | tf_op jit(solution)/shard_map/layer_one/pallas_call | solution.py:256
  70.5 1.2 collective-permute-start.1
  71.8 2.3 fusion.19.own_ref
  74.2 2.3 convolution_bitcast_fusion.pool_ref
  76.6 0.5 copy-done.7
  77.0 10.1 %layer_two.1 = (bf16[1024,1024]{1,0:T(8,128)(2,1)}, bf16[1024,1024]{1,0:T(8,128)(2,1)S(1)}, bf16[1024,1024]{1,0:T(8,128)(2,1)S(1)}, bf16[1024,1024]{1,0:T(8,128)(2,1)S(1)}, f32[128,1024]{1,0:T(8,128)S(1)}) custom-call(f32[1024,1024]{1,0:T(8,128)S(1)} %fusion.19.own_ref, f32[1024,1024]{1,0:T(8,128)S(1)} %convolution_bitcast_fusion.pool_ref, ...), custom_call_target="tpu_custom_call" | custom-call | tf_op jit(solution)/shard_map/layer_two/pallas_call | solution.py:321
  87.1 2.5 %fusion.7 = bf16[1024,1024]{1,0:T(8,128)(2,1)S(1)} fusion(bf16[1024,1024]{1,0:T(8,128)(2,1)S(1)} %get-tuple-element.36, bf16[1024,1024]{1,0:T(8,128)(2,1)S(1)} %get-tuple-element.48, bf16[1024,1024]{1,0:T(8,128)(2,1)S(1)} %get-tuple-element.31, pred[]{:T(512)S(6)} %eq.9), kind=kOutput, calls=%fused_computation.14 | convolution fusion | flops 2149580800 | bytes 8388609 | tf_op jit(solution)/shard_map/dot_general | solution.py:33
  89.7 7.0 %collective-permute-start.5 = (bf16[1024,1024]{1,0:T(8,128)(2,1)S(1)}, bf16[1024,1024]{1,0:T(8,128)(2,1)S(1)}, u32[]{:S(2)}, u32[]{:S(2)}) collective-permute-start(bf16[1024,1024]{1,0:T(8,128)(2,1)S(1)} %fusion.7), channel_id=1, source_target_pairs={{0,1},{1,0},{2,3},{3,2},{4,5},{5,4},{6,7},{7,6},{8,9},{9,8},{10,11... | collective-permute-start | bytes 6291464 | tf_op jit(solution)/shard_map/ppermute | solution.py:570
  96.8 1.7 collective-permute-start.2
  98.5 1.9 collective-permute-done.5
  100.4 4.0 %fusion = bf16[128,8,1024]{2,1,0:T(8,128)(2,1)} fusion(bf16[1024,1024]{1,0:T(8,128)(2,1)S(1)} %collective-permute-done.5, bf16[1024,1024]{1,0:T(8,128)(2,1)S(1)} %get-tuple-element.36, bf16[1024,1024]{1,0:T(8,128)(2,1)S(1)} %get-tuple-element.31, bf16[1024,1024]{1,0:T(8,128)(2,1)S(1)} %get-tuple-element.48, pred[]{:T(512)S(6)} %eq.9), kind=kOutput, calls=%fused_computation.5 | convolution fusion | flops 2151677952 | bytes 10485761 | tf_op jit(solution)/shard_map/dot_general | solution.py:33
  104.4 9.5 %all-to-all-start.3 = ((bf16[128,8,1024]{2,1,0:T(8,128)(2,1)}), bf16[128,8,1024]{2,1,0:T(8,128)(2,1)}, u32[]{:S(2)}, u32[]{:S(2)}) async-start(bf16[128,8,1024]{2,1,0:T(8,128)(2,1)} %fusion), calls=%async_computation.3 | async-start | bytes 4194304 | tf_op jit(solution)/shard_map/all_to_all | solution.py:560
  114.0 4.7 %fusion.20 = f32[1024,1024]{0,1:T(8,128)S(1)} fusion(bf16[1024,1024]{1,0:T(8,128)(2,1)} %get-tuple-element.38, bf16[1024,1024]{1,0:T(8,128)(2,1)} %copy-done.15), kind=kOutput, calls=%fused_computation.26 | convolution fusion | flops 2147483648 | bytes 8388608 | tf_op jit(solution)/shard_map/dot_general | solution.py:25
  118.7 2.4 %bitcast_add_fusion.gh_ref = f32[1024,1024]{1,0:T(8,128)S(1)} fusion(f32[1024,1024]{0,1:T(8,128)S(1)} %fusion.20, bf16[1024,1024]{1,0:T(8,128)(2,1)S(1)} %copy-done.14, bf16[1024,1024]{1,0:T(8,128)(2,1)S(1)} %copy-done), kind=kOutput, calls=%fused_computation | convolution fusion | flops 2148532224 | bytes 12582912 | tf_op jit(solution)/shard_map/dot_general | solution.py:29
  121.2 0.3 copy-done.4
  121.6 0.1 copy-done.6
  121.8 8.2 %back_one.1 = (bf16[1024,1024]{1,0:T(8,128)(2,1)}, bf16[2048,256]{1,0:T(8,128)(2,1)}) custom-call(f32[1024,1024]{1,0:T(8,128)S(1)} %bitcast_add_fusion.gh_ref, f32[64,1024]{1,0:T(8,128)S(1)} %collective-permute-done.2.first_ref, f32[64,1024]{1,0:T(8,128)S(1)} %collective-permute-done.3.last_ref, f32[1024,1024]{1,0:T(8,128)S(1)} %copy-done.2, ...), custom_call_target="tpu_custom_call" | custom-call | tf_op jit(solution)/shard_map/back_one/pallas_call | solution.py:408
  129.9 2.5 %convolution_convert_fusion = bf16[256,1024]{1,0:T(8,128)(2,1)S(1)} fusion(bf16[1024,1024]{1,0:T(8,128)(2,1)} %get-tuple-element.45, bf16[1024,256]{1,0:T(8,128)(2,1)S(1)} %copy-done.23, bf16[1024,256]{1,0:T(8,128)(2,1)S(1)} %copy-done.22, pred[]{:T(512)S(6)} %eq.9), kind=kOutput, calls=%fused_computation.17 | convolution fusion | flops 537395200 | bytes 3670017 | tf_op jit(solution)/shard_map/dot_general | solution.py:33
  132.5 1.4 collective-permute-start.4
  133.9 1.5 collective-permute-done.4
  135.4 0.7 fusion.12
  136.2 1.2 pad_maximum_fusion
  137.5 6.6 %all-to-all-done.3.parts_ref = bf16[128,8,1024]{2,1,0:T(8,128)(2,1)} async-done(((bf16[128,8,1024]{2,1,0:T(8,128)(2,1)}), bf16[128,8,1024]{2,1,0:T(8,128)(2,1)}, u32[]{:S(2)}, u32[]{:S(2)}) %all-to-all-start.3) | async-done | bytes 2097184 | tf_op jit(solution)/shard_map/all_to_all | solution.py:560
  144.1 4.4 %all-to-all-start.2 = ((bf16[128,24,256]{2,1,0:T(8,128)(2,1)}), bf16[128,24,256]{2,1,0:T(8,128)(2,1)S(1)}, u32[]{:S(2)}, u32[]{:S(2)}) async-start(bf16[128,24,256]{2,1,0:T(8,128)(2,1)} %pad_maximum_fusion), calls=%async_computation.2 | async-start | bytes 3145728 | tf_op jit(solution)/shard_map/all_to_all | solution.py:560
  148.5 1.7 two_sum.1.two_ref
  150.2 23.2 %all-to-all-done.2.got_ref = bf16[128,24,256]{2,1,0:T(8,128)(2,1)S(1)} async-done(((bf16[128,24,256]{2,1,0:T(8,128)(2,1)}), bf16[128,24,256]{2,1,0:T(8,128)(2,1)S(1)}, u32[]{:S(2)}, u32[]{:S(2)}) %all-to-all-start.2) | async-done | bytes 1572896 | tf_op jit(solution)/shard_map/all_to_all | solution.py:560
  173.5 1.1 copy-done.20
  174.6 3.6 %spread.1 = bf16[128,8,1280]{2,1,0:T(8,128)(2,1)} custom-call(bf16[2,8,1024]{2,1,0:T(8,128)(2,1)S(1)} %two_sum.1.two_ref, bf16[128,24,256]{2,1,0:T(8,128)(2,1)} %copy-done.20), custom_call_target="tpu_custom_call" | custom-call | tf_op jit(solution)/shard_map/spread/pallas_call | solution.py:545
  178.2 41.7 %all_to_all.32 = bf16[128,8,1280]{2,1,0:T(8,128)(2,1)} all-to-all(bf16[128,8,1280]{2,1,0:T(8,128)(2,1)} %spread.1), channel_id=1, replica_groups=mesh['grp'=4,'dom'=32] {'grp','dom'}, dimensions={0} | all-to-all | bytes 5242880 | tf_op jit(solution)/shard_map/all_to_all | solution.py:560
  219.9 1.0 collective-permute-start.6
  220.9 0.5 broadcast.4
  221.4 0.8 reduce.3
  222.2 0.1 reshape.76.inc_ref
  222.3 11.3 %update.1 = (f32[4096,256]{1,0:T(8,128)}, f32[8,1,512]{2,1,0:T(1,128)}) custom-call(s32[1,2048]{1,0:T(1,128)S(1)} %reshape.76.inc_ref, bf16[128,24,256]{2,1,0:T(8,128)(2,1)} %copy-done.20, f32[4096,256]{1,0:T(8,128)} %table_ref.3, f32[8,1,512]{2,1,0:T(1,128)S(1)} %bitcast.56), custom_call_target="tpu_custom_call" | custom-call | flops 4294967296 | bytes 4194304 | tf_op jit(solution)/shard_map/update/pallas_call | solution.py:470
  233.6 2.9 %broadcast_select_fusion = (bf16[128,8,1280]{2,1,0:T(8,128)(2,1)S(1)}, bf16[128,8,1280]{2,1,0:T(8,128)(2,1)S(1)}) fusion(bf16[128,8,1280]{2,1,0:T(8,128)(2,1)} %collective-permute-done.6, bf16[128,8,1280]{2,1,0:T(8,128)(2,1)} %all_to_all.32, pred[]{:T(512)S(6)} %eq.9), kind=kLoop, calls=%fused_computation.2 | loop fusion | flops 2621440 | bytes 10485761 | tf_op jit(solution)/shard_map/jit(_where)/select_n | solution.py:638
  236.6 2.6 %slice_bitcast_fusion = (bf16[1024,1024]{1,0:T(8,128)(2,1)}, bf16[1024,1024]{1,0:T(8,128)(2,1)}) fusion(bf16[128,8,1280]{2,1,0:T(8,128)(2,1)S(1)} %get-tuple-element.49, bf16[128,8,1280]{2,1,0:T(8,128)(2,1)S(1)} %get-tuple-element.50), kind=kLoop, calls=%fused_computation.6 | loop fusion | bytes 8388608 | tf_op jit(solution)/shard_map/reshape | solution.py:633
  239.2 0.9 copy.34
  240.0 0.9 copy.33
  (57 shorter events, 0.5 us)
Async XLA Ops:
  0.6 71.2 %copy-start = (bf16[1024,1024]{1,0:T(8,128)(2,1)S(1)}, bf16[1024,1024]{1,0:T(8,128)(2,1)}, u32[]{:S(2)}) copy-start(bf16[1024,1024]{1,0:T(8,128)(2,1)} %param.16) | copy-start | bytes 6291460
  0.6 0.8 copy-start.11
  1.5 0.7 copy-start.12
  37.9 4.6 %copy-start.16 = (s32[1024,8]{0,1:T(8,128)S(1)}, s32[1024,8]{0,1:T(8,128)}, u32[]{:S(2)}) copy-start(s32[1024,8]{0,1:T(8,128)} %param.21) | copy-start | bytes 98308
  37.9 23.8 %all-to-all-start.1 = ((bf16[128,16,256]{2,1,0:T(8,128)(2,1)}), bf16[128,16,256]{2,1,0:T(8,128)(2,1)S(1)}, u32[]{:S(2)}, u32[]{:S(2)}) async-start(bf16[128,16,256]{2,1,0:T(8,128)(2,1)} %bitcast.58), calls=%async_computation.1 | async-start | bytes 2097152 | tf_op jit(solution)/shard_map/all_to_all | solution.py:560
  42.5 4.5 %copy-start.17 = (s32[1024,8]{0,1:T(8,128)S(1)}, s32[1024,8]{0,1:T(8,128)}, u32[]{:S(2)}) copy-start(s32[1024,8]{0,1:T(8,128)} %param.22) | copy-start | bytes 98308
  47.0 15.7 %copy-start.10 = (s32[1024]{0:T(1024)S(1)}, s32[1024]{0:T(1024)}, u32[]{:S(2)}) copy-start(s32[1024]{0:T(1024)} %param.20) | copy-start | bytes 12292
  61.7 1.0 copy-start.21
  70.5 6.1 %collective-permute-start.1 = (bf16[64,1024]{1,0:T(8,128)(2,1)S(1)}, bf16[64,1024]{1,0:T(8,128)(2,1)S(1)}, u32[]{:S(2)}, u32[]{:S(2)}) collective-permute-start(bf16[64,1024]{1,0:T(8,128)(2,1)S(1)} %get-tuple-element.51), channel_id=1, source_target_pairs={{0,1},{1,2},{2,3},{3,4},{4,5},{5,6},{6,7},{7,8},{8,9},{9,10},{10,1... | collective-permute-start | bytes 393224 | tf_op jit(solution)/shard_map/ppermute | solution.py:600
  71.7 2.4 %copy-start.25 = (bf16[1024,1024]{1,0:T(8,128)(2,1)S(1)}, bf16[1024,1024]{1,0:T(8,128)(2,1)}, u32[]{:S(2)}) copy-start(bf16[1024,1024]{1,0:T(8,128)(2,1)} %get-tuple-element.32) | copy-start | bytes 6291460
  71.7 4.8 %collective-permute-start = (bf16[64,1024]{1,0:T(8,128)(2,1)S(1)}, bf16[64,1024]{1,0:T(8,128)(2,1)S(1)}, u32[]{:S(2)}, u32[]{:S(2)}) collective-permute-start(bf16[64,1024]{1,0:T(8,128)(2,1)S(1)} %get-tuple-element.52), channel_id=1, source_target_pairs={{1,0},{2,1},{3,2},{4,3},{5,4},{6,5},{7,6},{8,7},{9,8},{10,9},{11,1... | collective-permute-start | bytes 393224 | tf_op jit(solution)/shard_map/ppermute | solution.py:601
  74.2 2.4 copy-start.3
  74.2 2.9 %copy-start.7 = (bf16[1024,1024]{1,0:T(8,128)(2,1)S(1)}, bf16[1024,1024]{1,0:T(8,128)(2,1)}, u32[]{:S(2)}) copy-start(bf16[1024,1024]{1,0:T(8,128)(2,1)} %wn_ref.4) | copy-start | bytes 6291460
  74.2 2.9 %copy-start.8 = (bf16[128,1024]{1,0:T(8,128)(2,1)S(1)}, bf16[128,1024]{1,0:T(8,128)(2,1)}, u32[]{:S(2)}) copy-start(bf16[128,1024]{1,0:T(8,128)(2,1)} %get-tuple-element.34.edge_t_ref) | copy-start | bytes 786436
  74.2 2.9 %copy-start.9 = (bf16[1024,128]{1,0:T(8,128)(2,1)S(1)}, bf16[1024,128]{1,0:T(8,128)(2,1)}, u32[]{:S(2)}) copy-start(bf16[1024,128]{1,0:T(8,128)(2,1)} %get-tuple-element.33.edge_ref) | copy-start | bytes 786436
  87.1 2.5 %copy-start.15 = (bf16[1024,1024]{1,0:T(8,128)(2,1)}, bf16[1024,1024]{1,0:T(8,128)(2,1)S(1)}, u32[]{:S(2)}) copy-start(bf16[1024,1024]{1,0:T(8,128)(2,1)S(1)} %get-tuple-element.37) | copy-start | bytes 6291460
  87.1 13.3 %copy-start.13 = (bf16[1024,1024]{1,0:T(8,128)(2,1)}, bf16[1024,1024]{1,0:T(8,128)(2,1)S(1)}, u32[]{:S(2)}) copy-start(bf16[1024,1024]{1,0:T(8,128)(2,1)S(1)} %get-tuple-element.36) | copy-start | bytes 6291460
  89.7 10.8 %collective-permute-start.5 = (bf16[1024,1024]{1,0:T(8,128)(2,1)S(1)}, bf16[1024,1024]{1,0:T(8,128)(2,1)S(1)}, u32[]{:S(2)}, u32[]{:S(2)}) collective-permute-start(bf16[1024,1024]{1,0:T(8,128)(2,1)S(1)} %fusion.7), channel_id=1, source_target_pairs={{0,1},{1,0},{2,3},{3,2},{4,5},{5,4},{6,7},{7,6},{8,9},{9,8},{10,11... | collective-permute-start | bytes 6291464 | tf_op jit(solution)/shard_map/ppermute | solution.py:570
  96.7 24.5 %collective-permute-start.3 = (f32[64,1024]{1,0:T(8,128)S(1)}, f32[64,1024]{1,0:T(8,128)S(1)}, u32[]{:S(2)}, u32[]{:S(2)}) collective-permute-start(f32[64,1024]{1,0:T(8,128)S(1)} %get-tuple-element.53), channel_id=1, source_target_pairs={{1,0},{2,1},{3,2},{4,3},{5,4},{6,5},{7,6},{8,7},{9,8},{10,9},{11,1... | collective-permute-start | bytes 786440 | tf_op jit(solution)/shard_map/ppermute | solution.py:608
  96.8 24.4 %collective-permute-start.2 = (f32[64,1024]{1,0:T(8,128)S(1)}, f32[64,1024]{1,0:T(8,128)S(1)}, u32[]{:S(2)}, u32[]{:S(2)}) collective-permute-start(f32[64,1024]{1,0:T(8,128)S(1)} %get-tuple-element.54), channel_id=1, source_target_pairs={{0,1},{1,2},{2,3},{3,4},{4,5},{5,6},{6,7},{7,8},{8,9},{9,10},{10,1... | collective-permute-start | bytes 786440 | tf_op jit(solution)/shard_map/ppermute | solution.py:607
  104.4 39.6 %all-to-all-start.3 = ((bf16[128,8,1024]{2,1,0:T(8,128)(2,1)}), bf16[128,8,1024]{2,1,0:T(8,128)(2,1)}, u32[]{:S(2)}, u32[]{:S(2)}) async-start(bf16[128,8,1024]{2,1,0:T(8,128)(2,1)} %fusion), calls=%async_computation.3 | async-start | bytes 4194304 | tf_op jit(solution)/shard_map/all_to_all | solution.py:560
  114.0 4.7 %copy-start.14 = (bf16[1024,1024]{1,0:T(8,128)(2,1)S(1)}, bf16[1024,1024]{1,0:T(8,128)(2,1)}, u32[]{:S(2)}) copy-start(bf16[1024,1024]{1,0:T(8,128)(2,1)} %copy-done.13) | copy-start | bytes 6291460
  118.7 2.5 %copy-start.2 = (f32[1024,1024]{1,0:T(8,128)S(1)}, f32[1024,1024]{1,0:T(8,128)}, u32[]{:S(2)}) copy-start(f32[1024,1024]{1,0:T(8,128)} %get-tuple-element.40.before_ref) | copy-start | bytes 12582916
  118.7 2.9 %copy-start.4 = (bf16[1024,1024]{1,0:T(8,128)(2,1)S(1)}, bf16[1024,1024]{1,0:T(8,128)(2,1)}, u32[]{:S(2)}) copy-start(bf16[1024,1024]{1,0:T(8,128)(2,1)} %get-tuple-element.41.adj_t_ref) | copy-start | bytes 6291460
  118.7 2.9 %copy-start.5 = (bf16[256,1024]{1,0:T(8,128)(2,1)S(1)}, bf16[256,1024]{1,0:T(8,128)(2,1)}, u32[]{:S(2)}) copy-start(bf16[256,1024]{1,0:T(8,128)(2,1)} %ws_ref.3) | copy-start | bytes 1572868
  118.7 3.0 %copy-start.6 = (bf16[256,1024]{1,0:T(8,128)(2,1)S(1)}, bf16[256,1024]{1,0:T(8,128)(2,1)}, u32[]{:S(2)}) copy-start(bf16[256,1024]{1,0:T(8,128)(2,1)} %wn_ref.5) | copy-start | bytes 1572868
  121.7 8.2 %copy-start.22 = (bf16[1024,256]{1,0:T(8,128)(2,1)S(1)}, bf16[1024,256]{1,0:T(8,128)(2,1)}, u32[]{:S(2)}) copy-start(bf16[1024,256]{1,0:T(8,128)(2,1)} %get-tuple-element.43) | copy-start | bytes 1572868
  121.7 8.2 %copy-start.23 = (bf16[1024,256]{1,0:T(8,128)(2,1)S(1)}, bf16[1024,256]{1,0:T(8,128)(2,1)}, u32[]{:S(2)}) copy-start(bf16[1024,256]{1,0:T(8,128)(2,1)} %get-tuple-element.44) | copy-start | bytes 1572868
  129.9 5.5 %copy-start.19 = (bf16[1024,1024]{1,0:T(8,128)(2,1)S(1)}, bf16[1024,1024]{1,0:T(8,128)(2,1)}, u32[]{:S(2)}) copy-start(bf16[1024,1024]{1,0:T(8,128)(2,1)} %get-tuple-element.45) | copy-start | bytes 6291460
  132.4 3.8 %copy-start.24 = (bf16[2048,256]{1,0:T(8,128)(2,1)S(1)}, bf16[2048,256]{1,0:T(8,128)(2,1)}, u32[]{:S(2)}) copy-start(bf16[2048,256]{1,0:T(8,128)(2,1)} %get-tuple-element.42) | copy-start | bytes 3145732
  132.5 3.0 %collective-permute-start.4 = (bf16[256,1024]{1,0:T(8,128)(2,1)S(1)}, bf16[256,1024]{1,0:T(8,128)(2,1)S(1)}, u32[]{:S(2)}, u32[]{:S(2)}) collective-permute-start(bf16[256,1024]{1,0:T(8,128)(2,1)S(1)} %convolution_convert_fusion), channel_id=1, source_target_pairs={{0,1},{1,0},{2,3},{3,2},{4,5},{5,4},{6,7},{7,6},{8,9},{9,8},{10,11... | collective-permute-start | bytes 1572872 | tf_op jit(solution)/shard_map/ppermute | solution.py:570
  144.1 29.4 %all-to-all-start.2 = ((bf16[128,24,256]{2,1,0:T(8,128)(2,1)}), bf16[128,24,256]{2,1,0:T(8,128)(2,1)S(1)}, u32[]{:S(2)}, u32[]{:S(2)}) async-start(bf16[128,24,256]{2,1,0:T(8,128)(2,1)} %pad_maximum_fusion), calls=%async_computation.2 | async-start | bytes 3145728 | tf_op jit(solution)/shard_map/all_to_all | solution.py:560
  173.5 1.1 copy-start.20
  178.2 44.1 %copy-start.18 = (f32[4096]{0:T(1024)S(1)}, f32[4096]{0:T(1024)}, u32[]{:S(2)}) copy-start(f32[4096]{0:T(1024)} %param.13) | copy-start | bytes 49156
  219.9 13.7 %collective-permute-start.6 = (bf16[128,8,1280]{2,1,0:T(8,128)(2,1)}, bf16[128,8,1280]{2,1,0:T(8,128)(2,1)}, u32[]{:S(2)}, u32[]{:S(2)}) collective-permute-start(bf16[128,8,1280]{2,1,0:T(8,128)(2,1)} %all_to_all.32), channel_id=1, source_target_pairs={{0,1},{1,0},{2,3},{3,2},{4,5},{5,4},{6,7},{7,6},{8,9},{9,8},{10,11... | collective-permute-start | bytes 7864328 | tf_op jit(solution)/shard_map/ppermute | solution.py:625
  236.6 4.3 %copy-start.1 = (bf16[1024,1024]{1,0:T(8,128)(2,1)S(1)}, bf16[1024,1024]{1,0:T(8,128)(2,1)}, u32[]{:S(2)}) copy-start(bf16[1024,1024]{1,0:T(8,128)(2,1)} %param.16) | copy-start | bytes 6291460
where the time goes:
time: 242 us; the launch traced here: 241 us
  Pallas kernels  66.7 us (28%)
  blocking collectives  62.5 us (26%)
  waiting for transfers between devices  43.3 us (18%)
  starting transfers between devices  31.1 us (13%)
  matrix products  21.6 us (9%)
  local copies, waits for them, and re-layouts  9.8 us (4%)
  other arithmetic  4.92 us (2%)
    all_to_all x2, blocking collectives, exchange(): return lax.all_to_all(x, AXES, 0, 0, tiled=True)  62.5 us
    all_to_all x3, waiting for transfers between devices, exchange(): return lax.all_to_all(x, AXES, 0, 0, tiled=True)  39.8 us
    all_to_all x3, starting transfers between devices, exchange(): return lax.all_to_all(x, AXES, 0, 0, tiled=True)  18.5 us
    pallas_call x1, Pallas kernels, pick(): pl.pallas_call(pick_kernel, grid=(rows // block,), in_specs=[pl.BlockSpec...  14.2 us
    pallas_call x1, Pallas kernels, update(): pl.pallas_call(update_kernel, grid=(rows // block,), in_specs=[pl.BlockSp...  11.3 us
    pallas_call x1, Pallas kernels, layer_two(): pl.pallas_call(layer_two_kernel, grid=(nodes // block,), in_specs=[pl.Blo...  10.1 us
    dot_general x4, matrix products, tn(): lax.dot_general(a, b, (((0,), (0,)), ((), ())), preferred_element_type=F32)  9.75 us
    dot_general x3, matrix products, nn(): lax.dot_general(a, b, (((1,), (0,)), ((), ())), preferred_element_type=F32)  9.38 us
  transfers between devices with their start and end apart: 10, of which 5 were waited for; matrix products, arithmetic and copies ran while one was open for 9% of the time, Pallas kernels for 13%

commit v1 on v0

--- a/solution.py
+++ b/solution.py
@@ -102,7 +102,7 @@
         ),
         compiler_params=params(8),
         name="prep",
-    )(owner, row)
+    )(in_hbm(owner), in_hbm(row))
 
 
 def counts_kernel(shift, width, nbr_ref, *out_refs):
@@ -165,25 +165,14 @@
             col_ref[c * peers : (c + 1) * peers, :] = jnp.broadcast_to(
                 inc_ref[:, c : c + 1], (peers, 128)
             ).astype(I16)
-
-    def step(j, carry):
-        first = pl.multiple_of(j * 256, 256)
-        chunk = table_ref[pl.ds(first, 256), :].astype(BF)
-        base = (jnp.zeros(col_ref.shape, I32) + (i * rows + first)).astype(I16)
-        part = nn(hot_lanes(col_ref[...] - base, 256), chunk)
-        fresh = jnp.logical_and(i == 0, j == 0)
-
-        @pl.when(fresh)
-        def _():
-            acc_ref[...] = part
-
-        @pl.when(jnp.logical_not(fresh))
-        def _():
-            acc_ref[...] += part
-
-        return carry
-
-    lax.fori_loop(0, rows // 256, step, 0)
+        acc_ref[...] = jnp.zeros(acc_ref.shape, F32)
+
+    chunk = table_ref[...].astype(BF)
+    base = (jnp.zeros((512, 128), I32) + i * rows).astype(I16)
+
+    for at in range(0, acc_ref.shape[0], 512):
+        at = pl.ds(at, 512)
+        acc_ref[at, :] += nn(hot_lanes(col_ref[at, :] - base, rows), chunk)
 
     @pl.when(i == pl.num_programs(0) - 1)
     def _():
@@ -220,55 +209,95 @@
     )(incoming, in_hbm(table))
 
 
-def layer_one_kernel(
-    pos_ref, slot_ref, replies_ref, adj_ref, ws_ref, wn_ref,
-    selfs_ref, pooled_ref, before_ref, hidden_ref, fetched_ref,
+def nodes_of_one(slot_row, adj, fetched_ref, ws_ref, wn_ref):
+    self_hot = hot_lanes(to_lanes(slot_row), fetched_ref.shape[0])
+    selfs = nn(self_hot, fetched_ref[...]).astype(BF)
+    pooled = nn(adj, fetched_ref[...]).astype(BF)
+    before = nn(selfs, ws_ref[...]) + nn(pooled, wn_ref[...])
+    return selfs, pooled, before, (before * logistic(before)).astype(BF)
+
+
+def border_kernel(
+    pos_ref, slot_ref, replies_ref, head_ref, tail_ref, ws_ref, wn_ref,
+    fetched_ref, head_out_ref, tail_out_ref,
 ):
-    i = pl.program_id(0)
-    _, fetch = adj_ref.shape
-    slots = replies_ref.shape[0]
-
-    @pl.when(i == 0)
-    def _():
-        for at in range(0, fetch, 512):
-            place = hot_lanes(to_lanes(pos_ref[:, at : at + 512]), slots)
-            fetched_ref[at : at + 512, :] = nn(place, replies_ref[...]).astype(BF)
-
-    @pl.when(i > 0)
-    def _():
-        self_hot = hot_lanes(to_lanes(slot_ref[...]), fetch)
-        selfs = nn(self_hot, fetched_ref[...]).astype(BF)
-        pooled = nn(adj_ref[...], fetched_ref[...]).astype(BF)
-        selfs_ref[...] = selfs
-        pooled_ref[...] = pooled
-        before = nn(selfs, ws_ref[...]) + nn(pooled, wn_ref[...])
-        before_ref[...] = before
-        hidden_ref[...] = (before * logistic(before)).astype(BF)
-
-
-def layer_one(pos, slot, replies, adj, w_self, w_nbr):
+    fetch = fetched_ref.shape[0]
+    nodes = slot_ref.shape[1]
+    for at in range(0, fetch, 512):
+        place = hot_lanes(to_lanes(pos_ref[:, at : at + 512]), replies_ref.shape[0])
+        fetched_ref[at : at + 512, :] = nn(place, replies_ref[...]).astype(BF)
+    slots = jnp.concatenate([slot_ref[:, :BORDER], slot_ref[:, nodes - BORDER :]], axis=1)
+    adj = jnp.concatenate([head_ref[...], tail_ref[...]], axis=0)
+    hidden = nodes_of_one(slots, adj, fetched_ref, ws_ref, wn_ref)[3]
+    head_out_ref[...] = hidden[:BORDER]
+    tail_out_ref[...] = hidden[BORDER:]
+
+
+def border(pos, slot, replies, adj, w_self, w_nbr):
     nodes, fetch = adj.shape
     slots = replies.shape[0]
     emb, hid = w_self.shape
-    block = 512
-    late = lambda i: (jnp.maximum(i - 1, 0), 0)
     whole = lambda i: (0, 0)
     return pl.pallas_call(
-        layer_one_kernel,
-        grid=(1 + nodes // block,),
+        border_kernel,
+        grid=(1,),
         in_specs=[
             pl.BlockSpec((1, fetch), whole),
-            pl.BlockSpec((1, block), lambda i: (0, jnp.maximum(i - 1, 0))),
+            pl.BlockSpec((1, nodes), whole),
             pl.BlockSpec((slots, emb), whole),
-            pl.BlockSpec((block, fetch), late),
+            pl.BlockSpec((BORDER, fetch), whole),
+            pl.BlockSpec((BORDER, fetch), lambda i: (nodes // BORDER - 1, 0)),
             pl.BlockSpec((emb, hid), whole),
             pl.BlockSpec((emb, hid), whole),
         ],
         out_specs=[
-            pl.BlockSpec((block, emb), late),
-            pl.BlockSpec((block, emb), late),
-            pl.BlockSpec((block, hid), late),
-            pl.BlockSpec((block, hid), late),
+            pl.BlockSpec((fetch, emb), whole),
+            pl.BlockSpec((BORDER, hid), whole),
+            pl.BlockSpec((BORDER, hid), whole),
+        ],
+        out_shape=(
+            jax.ShapeDtypeStruct((fetch, emb), BF),
+            jax.ShapeDtypeStruct((BORDER, hid), BF),
+            jax.ShapeDtypeStruct((BORDER, hid), BF),
+        ),
+        compiler_params=params(24, "arbitrary"),
+        name="border",
+    )(pos, slot, replies, in_hbm(adj), in_hbm(adj), in_hbm(w_self), in_hbm(w_nbr))
+
+
+def layer_one_kernel(
+    slot_ref, fetched_ref, adj_ref, ws_ref, wn_ref, selfs_ref, pooled_ref, before_ref, hidden_ref
+):
+    selfs, pooled, before, hidden = nodes_of_one(
+        slot_ref[...], adj_ref[...], fetched_ref, ws_ref, wn_ref
+    )
+    selfs_ref[...] = selfs
+    pooled_ref[...] = pooled
+    before_ref[...] = before
+    hidden_ref[...] = hidden
+
+
+def layer_one(slot, fetched, adj, w_self, w_nbr):
+    nodes, fetch = adj.shape
+    emb, hid = w_self.shape
+    block = 256
+    rows = lambda i: (i, 0)
+    whole = lambda i: (0, 0)
+    return pl.pallas_call(
+        layer_one_kernel,
+        grid=(nodes // block,),
+        in_specs=[
+            pl.BlockSpec((1, block), lambda i: (0, i)),
+            pl.BlockSpec((fetch, emb), whole),
+            pl.BlockSpec((block, fetch), rows),
+            pl.BlockSpec((emb, hid), whole),
+            pl.BlockSpec((emb, hid), whole),
+        ],
+        out_specs=[
+            pl.BlockSpec((block, emb), rows),
+            pl.BlockSpec((block, emb), rows),
+            pl.BlockSpec((block, hid), rows),
+            pl.BlockSpec((block, hid), rows),
         ],
         out_shape=(
             pltpu.HBM((nodes, emb), BF),
@@ -276,41 +305,41 @@
             pltpu.HBM((nodes, hid), F32),
             jax.ShapeDtypeStruct((nodes, hid), BF),
         ),
-        scratch_shapes=[pltpu.VMEM((fetch, emb), BF)],
-        compiler_params=params(28, "arbitrary"),
+        compiler_params=params(20, "arbitrary"),
+        cost_estimate=cost(2 << 30),
         name="layer_one",
-    )(pos, slot, in_hbm(replies), in_hbm(adj), in_hbm(w_self), in_hbm(w_nbr))
+    )(slot, fetched, in_hbm(adj), in_hbm(w_self), in_hbm(w_nbr))
 
 
 def layer_two_kernel(
     own_ref, pool_ref, edge_ref, edge_t_ref, after_ref, before_in_ref, wn_ref, up_ref,
     emb_ref, pooled_ref, grad_ref, gpool_ref, gedge_ref,
 ):
-    i = pl.program_id(0)
+    block = own_ref.shape[0]
+
+    @pl.when(pl.program_id(0) == 0)
+    def _():
+        gedge_ref[...] = jnp.zeros(gedge_ref.shape, F32)
+
     halo = jnp.concatenate([after_ref[...], before_in_ref[...]], axis=0)
-    pooled = (pool_ref[...] + nn(edge_ref[...], halo)).astype(BF)
-    pooled_ref[...] = pooled
-    before = own_ref[...] + nn(pooled, wn_ref[...])
-    gate = logistic(before)
-    lifted = before * gate
-    scale = lax.rsqrt(jnp.mean(lifted * lifted, axis=1, keepdims=True) + epsilon)
-    normed = lifted * scale
-    emb_ref[...] = normed.astype(BF)
-    up = up_ref[...]
-    grad_lifted = scale * (up - normed * jnp.mean(up * normed, axis=1, keepdims=True))
-    grad = (grad_lifted * (gate + lifted * (1.0 - gate))).astype(BF)
-    grad_ref[...] = grad
-    gpool = nt(grad, wn_ref[...]).astype(BF)
-    gpool_ref[...] = gpool
-    part = nn(edge_t_ref[...], gpool)
-
-    @pl.when(i == 0)
-    def _():
-        gedge_ref[...] = part
-
-    @pl.when(i > 0)
-    def _():
-        gedge_ref[...] += part
+    half = 256
+    for at in range(0, block, half):
+        rows = pl.ds(at, half)
+        pooled = (pool_ref[rows, :] + nn(edge_ref[rows, :], halo)).astype(BF)
+        pooled_ref[rows, :] = pooled
+        before = own_ref[rows, :] + nn(pooled, wn_ref[...])
+        gate = logistic(before)
+        lifted = before * gate
+        scale = lax.rsqrt(jnp.mean(lifted * lifted, axis=1, keepdims=True) + epsilon)
+        normed = lifted * scale
+        emb_ref[rows, :] = normed.astype(BF)
+        up = up_ref[rows, :]
+        grad_lifted = scale * (up - normed * jnp.mean(up * normed, axis=1, keepdims=True))
+        grad = (grad_lifted * (gate + lifted * (1.0 - gate))).astype(BF)
+        grad_ref[rows, :] = grad
+        gpool = nt(grad, wn_ref[...]).astype(BF)
+        gpool_ref[rows, :] = gpool
+        gedge_ref[...] += nn(edge_t_ref[:, rows], gpool)
 
 
 def layer_two(own, pool, edge, edge_t, after, before, w_nbr, upstream):
@@ -363,6 +392,7 @@
     @pl.when(i == 0)
     def _():
         gh_scr[0:BORDER, :] += first_ref[...]
+        acc_ref[...] = jnp.zeros(acc_ref.shape, F32)
 
     @pl.when(i == last)
     def _():
@@ -377,15 +407,7 @@
     low = (gself - high.astype(F32)).astype(BF)
     gpool = nt(grad, wn_ref[...]).astype(BF)
     self_t = hot_rows(slot_ref[...], fetch, 0)
-    part = nn(self_t, high) + nn(self_t, low) + nn(adj_t_ref[...], gpool)
-
-    @pl.when(i == 0)
-    def _():
-        acc_ref[...] = part
-
-    @pl.when(i > 0)
-    def _():
-        acc_ref[...] += part
+    acc_ref[...] += nn(self_t, high) + nn(self_t, low) + nn(adj_t_ref[...], gpool)
 
     @pl.when(i == last)
     def _():
@@ -430,7 +452,9 @@
         scratch_shapes=[pltpu.VMEM((block, hid), F32), pltpu.VMEM((fetch, emb), F32)],
         compiler_params=params(24, "arbitrary"),
         name="back_one",
-    )(gh, first, last, before, slot, adj_t, w_self, w_nbr, pos)
+    )(
+        gh, first, last, in_hbm(before), slot, in_hbm(adj_t), in_hbm(w_self), in_hbm(w_nbr), pos,
+    )
 
 
 def update_kernel(
@@ -519,41 +543,115 @@
     )(in_hbm(parts))
 
 
-def spread_kernel(two_ref, got_ref, out_ref):
-    i = pl.program_id(0)
-    peers = out_ref.shape[0]
-    last = pl.num_programs(0) - 1
-
-    @pl.when(i < last)
-    def _():
-        for core in range(2):
-            for at in range(core, peers, 2):
-                out_ref[at] = two_ref[core]
-
-    @pl.when(i == last)
-    def _():
-        for core in range(2):
-            total = chip_sums(got_ref, core)
-            for at in range(core, peers, 2):
-                out_ref[at] = total
-
-
-def spread(two, got):
+def spread_two_kernel(two_ref, out_ref):
+    for core in range(2):
+        for at in range(core, out_ref.shape[0], 2):
+            out_ref[at] = two_ref[core]
+
+
+def spread_one_kernel(got_ref, rest_ref, out_ref):
+    for core in range(2):
+        total = chip_sums(got_ref, core)
+        for at in range(core, out_ref.shape[0], 2):
+            out_ref[at] = total
+
+
+def spread_two(two, peers, lanes):
     rows, width = two.shape[1:]
-    peers, held, lanes = got.shape
-    steps = width // lanes
-    return pl.pallas_call(
-        spread_kernel,
-        grid=(steps + 1,),
-        in_specs=[
-            pl.BlockSpec((2, rows, lanes), lambda i: (0, 0, jnp.minimum(i, steps - 1))),
-            pl.BlockSpec((peers, rows, lanes), lambda i: (0, held // rows - 1, 0)),
-        ],
+    return pl.pallas_call(
+        spread_two_kernel,
+        grid=(width // lanes,),
+        in_specs=[pl.BlockSpec((2, rows, lanes), lambda i: (0, 0, i))],
         out_specs=pl.BlockSpec((peers, rows, lanes), lambda i: (0, 0, i)),
         out_shape=pltpu.HBM((peers, rows, width + lanes), BF),
         compiler_params=params(8, "arbitrary"),
-        name="spread",
-    )(two, in_hbm(got))
+        cost_estimate=cost(1 << 30),
+        name="spread_two",
+    )(two)
+
+
+def spread_one(got, rest):
+    peers, held, lanes = got.shape
+    rows, width = rest.shape[1:]
+    return pl.pallas_call(
+        spread_one_kernel,
+        grid=(1,),
+        in_specs=[
+            pl.BlockSpec((peers, rows, lanes), lambda i: (0, held // rows - 1, 0)),
+            pl.BlockSpec(memory_space=pl.ANY),
+        ],
+        out_specs=pl.BlockSpec((peers, rows, lanes), lambda i: (0, 0, width // lanes - 1)),
+        out_shape=pltpu.HBM(rest.shape, BF),
+        input_output_aliases={1: 0},
+        compiler_params=params(8, "arbitrary"),
+        name="spread_one",
+    )(in_hbm(got), rest)
+
+
+SETTLE_CHUNKS = 4
+
+
+def settle_kernel(which_ref, mine_ref, *refs):
+    outs, buffer_ref, sem_in, sem_out = refs[-7:-3], refs[-3], refs[-2], refs[-1]
+    lanes = outs[2].shape[2]
+    peers, _, total = buffer_ref.shape
+    width = total - lanes
+    part = peers // SETTLE_CHUNKS
+
+    def fetch(q):
+        rows = pl.ds(q * part, part)
+        return pltpu.make_async_copy(mine_ref.at[rows], buffer_ref.at[rows], sem_in.at[q])
+
+    for q in range(SETTLE_CHUNKS):
+        fetch(q).start()
+    for core in range(2):
+
+        @pl.when(which_ref[0] == core)
+        def _():
+            one_ref, two_ref = outs[core], outs[2 + core]
+            moves = []
+            for q in range(SETTLE_CHUNKS):
+                fetch(q).wait()
+                rows = pl.ds(q * part, part)
+                moves.append(
+                    pltpu.make_async_copy(
+                        buffer_ref.at[rows, :, pl.ds(0, lanes)], two_ref.at[rows], sem_out.at[q, 0]
+                    )
+                )
+                moves.append(
+                    pltpu.make_async_copy(
+                        buffer_ref.at[rows, :, pl.ds(lanes, width)],
+                        one_ref.at[:, :, pl.ds(q * width, width)],
+                        sem_out.at[q, 1],
+                    )
+                )
+                moves[-2].start()
+                moves[-1].start()
+            for move in moves:
+                move.wait()
+
+
+def settle(which, mine, before):
+    peers, rows, total = mine.shape
+    lanes = 1024
+    width = total - lanes
+    assert lanes // width == SETTLE_CHUNKS
+    one = pltpu.HBM((peers // SETTLE_CHUNKS, rows, lanes), BF)
+    two = pltpu.HBM((peers, rows, lanes), BF)
+    hbm = pl.BlockSpec(memory_space=pl.ANY)
+    return pl.pallas_call(
+        settle_kernel,
+        in_specs=[pl.BlockSpec(memory_space=pltpu.SMEM), hbm] + [hbm] * len(before),
+        out_specs=[hbm] * 4,
+        out_shape=[one, one, two, two],
+        input_output_aliases={2 + k: k for k in range(len(before))},
+        scratch_shapes=[
+            pltpu.VMEM(mine.shape, BF),
+            pltpu.SemaphoreType.DMA((SETTLE_CHUNKS,)),
+            pltpu.SemaphoreType.DMA((SETTLE_CHUNKS, 2)),
+        ],
+        compiler_params=params(8),
+    )(which, in_hbm(mine), *before)
 
 
 def exchange(x):
@@ -568,7 +666,7 @@
     first_core = lax.axis_index("dom") % 2 == 0
     theirs = tn(jnp.where(first_core, right, left), grad).astype(BF)
     arrived = lax.ppermute(theirs, "dom", core_pairs())
-    ours = tn(jnp.where(first_core, left, right), grad)
+    ours = lax.optimization_barrier(tn(jnp.where(first_core, left, right), grad))
     return (ours + arrived.astype(F32)).astype(BF)
 
 
@@ -594,11 +692,12 @@
     adj_t, adj = counts(nbr_one.T, (count,), 0)
     inc_row = incoming.reshape(1, slots)
 
-    selfs, pooled_one, before_one, hidden = layer_one(
+    fetched, head, tail = border(
         pos, slot_row, replies.reshape(slots, emb), adj, w_self1, w_nbr1
     )
-    before = lax.ppermute(hidden[nodes - BORDER :], AXES, ring_up)
-    after = lax.ppermute(hidden[:BORDER], AXES, ring_down)
+    before = lax.ppermute(tail, AXES, ring_up)
+    after = lax.ppermute(head, AXES, ring_down)
+    selfs, pooled_one, before_one, hidden = layer_one(slot_row, fetched, adj, w_self1, w_nbr1)
     own = nn(hidden, w_self2)
     pool = nn(mid, hidden)
     embedded, pooled_two, grad_two, grad_pool, grad_edge = layer_two(
@@ -620,23 +719,16 @@
         [grad_slots.reshape(devices, cap, emb), tiles.reshape(devices, 8, emb)], axis=1
     )
     got = exchange(sent)
-    mine = exchange(spread(two_sum(parts_two), got))
+    rest = spread_two(two_sum(parts_two), devices, emb)
+    mine = exchange(spread_one(got, rest))
     new_table, new_accum = update(inc_row, got, table, accum)
     other = lax.ppermute(mine, "dom", core_pairs())
-    first_core = lax.axis_index("dom") % 2 == 0
-
-    def of_one(x):
-        x = x[:, :, hid:].reshape(across, down, 8, emb).transpose(1, 2, 0, 3)
-        return x.reshape(chip_one.shape)
-
-    def of_two(x):
-        return x[:, :, :hid].reshape(chip_two.shape)
-
-    grads = []
-    for of in (of_one, of_two):
-        grads.append(of(jnp.where(first_core, mine, other)))
-        grads.append(of(jnp.where(first_core, other, mine)))
-    return (embedded, new_table, new_accum) + tuple(grads)
+    core = lax.axis_index("dom") % 2
+    grads = settle(core.reshape(1), mine, ())
+    grads = settle((1 - core).reshape(1), other, grads)
+    shapes = (chip_one.shape, chip_one.shape, chip_two.shape, chip_two.shape)
+    grads = tuple(g.reshape(shape) for g, shape in zip(grads, shapes))
+    return (embedded, new_table, new_accum) + grads
 
 
 def solution(mesh):

time: 242 us -> 229 us (0.946)
  local copies, waits for them, and re-layouts: 9.8 us -> 1.47 us
  waiting for transfers between devices: 43.3 us -> 38.2 us
  Pallas kernels: 66.7 us -> 70.1 us
    pallas_call x2 -> x6, Pallas kernels: 11.4 us -> 18.8 us  [the longest x1 6.42 us: layer_one(): pl.pallas_call(layer_one_kernel, grid=(nodes // block,), in_specs=[pl.Blo...]
    ppermute x2, starting transfers between devices: 8.41 us -> 1.31 us  [chip_grads(): arrived = lax.ppermute(theirs, 'dom', core_pairs())]
    all_to_all x3, starting transfers between devices: 18.5 us -> 23.9 us  [exchange(): return lax.all_to_all(x, AXES, 0, 0, tiled=True)]
    pallas_call x1, Pallas kernels: 14.2 us -> 9.02 us  [pick(): pl.pallas_call(pick_kernel, grid=(rows // block,), in_specs=[pl.BlockSpec...]
    unnamed x52 -> x34, local copies, waits for them, and re-layouts: 4.72 us -> 0.79 us
    select_n x1 -> x0, other arithmetic: 2.87 us -> none  [local(): grads.append(of(jnp.where(first_core, other, mine)))]
    ppermute x2, waiting for transfers between devices: 3.47 us -> 0.79 us  [chip_grads(): arrived = lax.ppermute(theirs, 'dom', core_pairs())]
    reshape x1 -> x0, local copies, waits for them, and re-layouts: 2.6 us -> none  [of_two(): return x[:, :, :hid].reshape(chip_two.shape)]
  transfers between devices with their start and end apart: 10 -> 10, of which waited for: 5 -> 4; matrix products, arithmetic and copies ran while one was open for 9% -> 10% of each run, Pallas kernels for 13% -> 19%
where the time goes in v1:
time: 229 us; the launch traced here: 228 us
  Pallas kernels  70.1 us (31%)
  blocking collectives  62.5 us (27%)
  waiting for transfers between devices  38.2 us (17%)
  starting transfers between devices  29.9 us (13%)
  matrix products  19.9 us (9%)
  other arithmetic  4.34 us (2%)
    all_to_all x2, blocking collectives, exchange(): return lax.all_to_all(x, AXES, 0, 0, tiled=True)  62.5 us
    all_to_all x3, waiting for transfers between devices, exchange(): return lax.all_to_all(x, AXES, 0, 0, tiled=True)  37.4 us
    all_to_all x3, starting transfers between devices, exchange(): return lax.all_to_all(x, AXES, 0, 0, tiled=True)  23.9 us
    pallas_call x1, Pallas kernels, update(): pl.pallas_call(update_kernel, grid=(rows // block,), in_specs=[pl.BlockSp...  11.3 us
    pallas_call x1, Pallas kernels, back_one(): pl.pallas_call(back_one_kernel, grid=(nodes // block,), in_specs=[pl.Bloc...  9.66 us
    dot_general x3, matrix products, nn(): lax.dot_general(a, b, (((1,), (0,)), ((), ())), preferred_element_type=F32)  9.35 us
    pallas_call x2, Pallas kernels, counts(): pl.pallas_call(lambda *refs: counts_kernel(shift, sum(widths), *refs), gr...  9.18 us
    pallas_call x1, Pallas kernels, pick(): pl.pallas_call(pick_kernel, grid=(rows // block,), in_specs=[pl.BlockSpec...  9.02 us
  transfers between devices with their start and end apart: 10, of which 4 were waited for; matrix products, arithmetic and copies ran while one was open for 10% of the time, Pallas kernels for 19%

profile of v1, /device:TPU:1, one launch (start us, length us, event | category | flops | bytes accessed | tf_op | source)
XLA Modules:
  0.0 227.6 jit_solution(3674052595564907798)
XLA Ops:
  0.6 0.0 copy-start
  0.6 1.5 prep.1
  2.2 20.8 %all_to_all.31 = s32[128,1,16]{2,1,0:T(1,128)S(1)} all-to-all(s32[128,1,16]{2,1,0:T(1,128)S(1)} %bitcast.44), channel_id=1, replica_groups=mesh['grp'=4,'dom'=32] {'grp','dom'}, dimensions={0} | all-to-all | bytes 16384 | tf_op jit(solution)/shard_map/all_to_all | solution.py:658
  23.0 9.0 %pick.1 = bf16[2048,256]{1,0:T(8,128)(2,1)} custom-call(s32[128,16]{1,0:T(8,128)S(1)} %bitcast.43, f32[4096,256]{1,0:T(8,128)} %table_ref.3), custom_call_target="tpu_custom_call" | custom-call | tf_op jit(solution)/shard_map/pick/pallas_call | solution.py:193
  32.0 4.6 %all-to-all-start.1 = ((bf16[128,16,256]{2,1,0:T(8,128)(2,1)}), bf16[128,16,256]{2,1,0:T(8,128)(2,1)S(1)}, u32[]{:S(2)}, u32[]{:S(2)}) async-start(bf16[128,16,256]{2,1,0:T(8,128)(2,1)} %bitcast.51), calls=%async_computation.1 | async-start | bytes 2097152 | tf_op jit(solution)/shard_map/all_to_all | solution.py:658
  36.7 4.5 %shard_map.171 = (bf16[1024,1024]{1,0:T(8,128)(2,1)}, bf16[1024,1024]{1,0:T(8,128)(2,1)}) custom-call(s32[8,1024]{1,0:T(8,128)S(1)} %bitcast.48), custom_call_target="tpu_custom_call" | custom-call | flops 4294967296 | bytes 4194304 | tf_op jit(solution)/shard_map/pallas_call | solution.py:146
  41.2 4.7 %shard_map.172 = (bf16[1024,1024]{1,0:T(8,128)(2,1)}, bf16[1024,1024]{1,0:T(8,128)(2,1)}, bf16[128,1024]{1,0:T(8,128)(2,1)}, bf16[1024,128]{1,0:T(8,128)(2,1)}) custom-call(s32[8,1024]{1,0:T(8,128)S(1)} %bitcast.49), custom_call_target="tpu_custom_call" | custom-call | flops 4294967296 | bytes 4194304 | tf_op jit(solution)/shard_map/pallas_call | solution.py:146
  45.8 10.0 %all-to-all-done.1 = bf16[128,16,256]{2,1,0:T(8,128)(2,1)S(1)} async-done(((bf16[128,16,256]{2,1,0:T(8,128)(2,1)}), bf16[128,16,256]{2,1,0:T(8,128)(2,1)S(1)}, u32[]{:S(2)}, u32[]{:S(2)}) %all-to-all-start.1) | async-done | bytes 1048608 | tf_op jit(solution)/shard_map/all_to_all | solution.py:658
  55.9 3.2 %border.1 = (bf16[1024,256]{1,0:T(8,128)(2,1)S(1)}, bf16[64,1024]{1,0:T(8,128)(2,1)S(1)}, bf16[64,1024]{1,0:T(8,128)(2,1)S(1)}) custom-call(s32[1,1024]{1,0:T(1,128)S(1)} %get-tuple-element.39.pos_ref, s32[1,1024]{1,0:T(1,128)S(1)} %bitcast.45, bf16[2048,256]{1,0:T(8,128)(2,1)S(1)} %bitcast.42, ...), custom_call_target="tpu_custom_call" | custom-call | tf_op jit(solution)/shard_map/border/pallas_call | solution.py:241
  59.1 1.0 collective-permute-start
  60.1 0.8 collective-permute-start.1
  60.9 6.4 %layer_one.1 = (bf16[1024,256]{1,0:T(8,128)(2,1)}, bf16[1024,256]{1,0:T(8,128)(2,1)}, f32[1024,1024]{1,0:T(8,128)}, bf16[1024,1024]{1,0:T(8,128)(2,1)S(1)}) custom-call(s32[1,1024]{1,0:T(1,128)S(1)} %bitcast.46, bf16[1024,256]{1,0:T(8,128)(2,1)S(1)} %get-tuple-element.42.fetched_ref, bf16[1024,1024]{1,0:T(8,128)(2,1)} %get-tuple-element.41.head_ref.tail_ref.adj_ref, ...), custom_call_target="tpu_custom_call" | custom-call | flops 2147483648 | bytes 4194304 | tf_op jit(solution)/shard_map/layer_one/pallas_call | solution.py:286
  67.3 2.3 %fusion.16.own_ref = f32[1024,1024]{1,0:T(8,128)S(1)} fusion(bf16[1024,1024]{1,0:T(8,128)(2,1)S(1)} %get-tuple-element.43, bf16[1024,1024]{1,0:T(8,128)(2,1)S(1)} %copy-done), kind=kOutput, calls=%fused_computation.20 | convolution fusion | flops 2147483648 | bytes 8388608 | tf_op jit(solution)/shard_map/dot_general | solution.py:25
  69.7 2.3 %convolution_bitcast_fusion.pool_ref = f32[1024,1024]{1,0:T(8,128)S(1)} fusion(bf16[1024,1024]{1,0:T(8,128)(2,1)S(1)} %copy-done.16, bf16[1024,1024]{1,0:T(8,128)(2,1)S(1)} %get-tuple-element.43), kind=kOutput, calls=%fused_computation.2 | convolution fusion | flops 2147483648 | bytes 8388608 | tf_op jit(solution)/shard_map/dot_general | solution.py:25
  72.1 0.5 copy-done.2
  72.5 0.0 copy-done.4
  72.6 8.9 %layer_two.1 = (bf16[1024,1024]{1,0:T(8,128)(2,1)}, bf16[1024,1024]{1,0:T(8,128)(2,1)S(1)}, bf16[1024,1024]{1,0:T(8,128)(2,1)S(1)}, bf16[1024,1024]{1,0:T(8,128)(2,1)S(1)}, f32[128,1024]{1,0:T(8,128)S(1)}) custom-call(f32[1024,1024]{1,0:T(8,128)S(1)} %fusion.16.own_ref, f32[1024,1024]{1,0:T(8,128)S(1)} %convolution_bitcast_fusion.pool_ref, ...), custom_call_target="tpu_custom_call" | custom-call | tf_op jit(solution)/shard_map/layer_two/pallas_call | solution.py:350
  81.5 2.5 %fusion.7 = bf16[1024,1024]{1,0:T(8,128)(2,1)S(1)} fusion(bf16[1024,1024]{1,0:T(8,128)(2,1)S(1)} %get-tuple-element.50, bf16[1024,1024]{1,0:T(8,128)(2,1)S(1)} %get-tuple-element.62, bf16[1024,1024]{1,0:T(8,128)(2,1)S(1)} %get-tuple-element.43, pred[]{:T(512)S(6)} %eq.8), kind=kOutput, calls=%fused_computation.10 | convolution fusion | flops 2149580800 | bytes 8388609 | tf_op jit(solution)/shard_map/dot_general | solution.py:33
  84.0 0.1 collective-permute-start.5
  84.1 0.6 collective-permute-start.3
  84.7 1.3 collective-permute-start.2
  85.9 2.5 %fusion.3 = f32[1024,1024]{1,0:T(8,128)S(1)} fusion(bf16[1024,1024]{1,0:T(8,128)(2,1)S(1)} %get-tuple-element.50, bf16[1024,1024]{1,0:T(8,128)(2,1)S(1)} %get-tuple-element.43, bf16[1024,1024]{1,0:T(8,128)(2,1)S(1)} %get-tuple-element.62, pred[]{:T(512)S(6)} %eq.8), kind=kOutput, calls=%fused_computation.6 | convolution fusion | flops 2148532224 | bytes 10485761 | tf_op jit(solution)/shard_map/dot_general | solution.py:33
  88.4 2.2 fusion
  90.6 13.9 %all-to-all-start.3 = ((bf16[128,8,1024]{2,1,0:T(8,128)(2,1)}), bf16[128,8,1024]{2,1,0:T(8,128)(2,1)}, u32[]{:S(2)}, u32[]{:S(2)}) async-start(bf16[128,8,1024]{2,1,0:T(8,128)(2,1)} %fusion), calls=%async_computation.3 | async-start | bytes 4194304 | tf_op jit(solution)/shard_map/all_to_all | solution.py:658
  104.5 4.7 %fusion.17 = f32[1024,1024]{0,1:T(8,128)S(1)} fusion(bf16[1024,1024]{1,0:T(8,128)(2,1)} %get-tuple-element.52, bf16[1024,1024]{1,0:T(8,128)(2,1)} %copy-done.8), kind=kOutput, calls=%fused_computation.21 | convolution fusion | flops 2147483648 | bytes 8388608 | tf_op jit(solution)/shard_map/dot_general | solution.py:25
  109.2 2.4 %bitcast_add_fusion.gh_ref = f32[1024,1024]{1,0:T(8,128)S(1)} fusion(f32[1024,1024]{0,1:T(8,128)S(1)} %fusion.17, bf16[1024,1024]{1,0:T(8,128)(2,1)S(1)} %copy-done.7, bf16[1024,1024]{1,0:T(8,128)(2,1)S(1)} %copy-done), kind=kOutput, calls=%fused_computation | convolution fusion | flops 2148532224 | bytes 12582912 | tf_op jit(solution)/shard_map/dot_general | solution.py:29
  111.6 9.7 %back_one.1 = (bf16[1024,1024]{1,0:T(8,128)(2,1)}, bf16[2048,256]{1,0:T(8,128)(2,1)}) custom-call(f32[1024,1024]{1,0:T(8,128)S(1)} %bitcast_add_fusion.gh_ref, f32[64,1024]{1,0:T(8,128)S(1)} %collective-permute-done.2.first_ref, f32[64,1024]{1,0:T(8,128)S(1)} %collective-permute-done.3.last_ref, f32[1024,1024]{1,0:T(8,128)} %get-tuple-element.54.before_ref, ...), custom_call_target="tpu_custom_call" | custom-call | tf_op jit(solution)/shard_map/back_one/pallas_call | solution.py:430
  121.3 2.5 %convolution_convert_fusion = bf16[256,1024]{1,0:T(8,128)(2,1)S(1)} fusion(bf16[1024,1024]{1,0:T(8,128)(2,1)} %get-tuple-element.59, bf16[1024,256]{1,0:T(8,128)(2,1)S(1)} %copy-done.14, bf16[1024,256]{1,0:T(8,128)(2,1)S(1)} %copy-done.13, pred[]{:T(512)S(6)} %eq.8), kind=kOutput, calls=%fused_computation.12 | convolution fusion | flops 537395200 | bytes 3670017 | tf_op jit(solution)/shard_map/dot_general | solution.py:33
  123.8 1.2 collective-permute-start.4
  125.0 0.7 fusion.11
  125.7 0.8 collective-permute-done.4
  126.5 0.1 add_convert_fusion.1
  126.7 0.2 copy-done.15
  127.0 1.2 pad_maximum_fusion
  128.2 6.4 %all-to-all-done.3.parts_ref = bf16[128,8,1024]{2,1,0:T(8,128)(2,1)} async-done(((bf16[128,8,1024]{2,1,0:T(8,128)(2,1)}), bf16[128,8,1024]{2,1,0:T(8,128)(2,1)}, u32[]{:S(2)}, u32[]{:S(2)}) %all-to-all-start.3) | async-done | bytes 2097184 | tf_op jit(solution)/shard_map/all_to_all | solution.py:658
  134.6 5.4 %all-to-all-start.2 = ((bf16[128,24,256]{2,1,0:T(8,128)(2,1)}), bf16[128,24,256]{2,1,0:T(8,128)(2,1)}, u32[]{:S(2)}, u32[]{:S(2)}) async-start(bf16[128,24,256]{2,1,0:T(8,128)(2,1)} %pad_maximum_fusion), calls=%async_computation.2 | async-start | bytes 3145728 | tf_op jit(solution)/shard_map/all_to_all | solution.py:658
  140.0 1.7 two_sum.1.two_ref
  141.7 1.9 spread_two.1.rest_ref
  143.6 21.1 %all-to-all-done.2.got_ref = bf16[128,24,256]{2,1,0:T(8,128)(2,1)} async-done(((bf16[128,24,256]{2,1,0:T(8,128)(2,1)}), bf16[128,24,256]{2,1,0:T(8,128)(2,1)}, u32[]{:S(2)}, u32[]{:S(2)}) %all-to-all-start.2) | async-done | bytes 1572896 | tf_op jit(solution)/shard_map/all_to_all | solution.py:658
  164.7 1.9 spread_one.1
  166.6 41.6 %all_to_all.32.mine_ref = bf16[128,8,1280]{2,1,0:T(8,128)(2,1)} all-to-all(bf16[128,8,1280]{2,1,0:T(8,128)(2,1)} %spread_one.1), channel_id=1, replica_groups=mesh['grp'=4,'dom'=32] {'grp','dom'}, dimensions={0} | all-to-all | bytes 5242880 | tf_op jit(solution)/shard_map/all_to_all | solution.py:658
  208.3 1.0 collective-permute-start.6
  209.3 0.5 broadcast.4
  209.8 0.8 reduce.3
  210.6 0.1 reshape.76.inc_ref
  210.7 11.3 %update.1 = (f32[4096,256]{1,0:T(8,128)}, f32[8,1,512]{2,1,0:T(1,128)}) custom-call(s32[1,2048]{1,0:T(1,128)S(1)} %reshape.76.inc_ref, bf16[128,24,256]{2,1,0:T(8,128)(2,1)} %all-to-all-done.2.got_ref, f32[4096,256]{1,0:T(8,128)} %table_ref.3, f32[8,1,512]{2,1,0:T(1,128)S(1)} %bitcast.50), custom_call_target="tpu_custom_call" | custom-call | flops 4294967296 | bytes 4194304 | tf_op jit(solution)/shard_map/update/pallas_call | solution.py:494
  222.0 2.7 %shard_map.173 = (bf16[32,8,1024]{2,1,0:T(8,128)(2,1)}, bf16[32,8,1024]{2,1,0:T(8,128)(2,1)}, bf16[128,8,1024]{2,1,0:T(8,128)(2,1)}, bf16[128,8,1024]{2,1,0:T(8,128)(2,1)}) custom-call(s32[1]{0:T(128)} %bitcast.20.which_ref, bf16[128,8,1280]{2,1,0:T(8,128)(2,1)} %all_to_all.32.mine_ref), custom_call_target="tpu_custom_call" | custom-call | tf_op jit(solution)/shard_map/pallas_call | solution.py:642
  224.7 2.7 %shard_map.174 = (bf16[32,8,1024]{2,1,0:T(8,128)(2,1)}, bf16[32,8,1024]{2,1,0:T(8,128)(2,1)}, bf16[128,8,1024]{2,1,0:T(8,128)(2,1)}, bf16[128,8,1024]{2,1,0:T(8,128)(2,1)}) custom-call(s32[1]{0:T(128)} %bitcast.18.which_ref, ...), custom_call_target="tpu_custom_call", output_to_operand_aliasing={{0}: (2, {}), {1}: (3, {}), {2}: (4, {}), {3}: (5, {})} | custom-call | tf_op jit(solution)/shard_map/pallas_call | solution.py:642
  (38 shorter events, 0.2 us)
Async XLA Ops:
  0.6 66.7 %copy-start = (bf16[1024,1024]{1,0:T(8,128)(2,1)S(1)}, bf16[1024,1024]{1,0:T(8,128)(2,1)}, u32[]{:S(2)}) copy-start(bf16[1024,1024]{1,0:T(8,128)(2,1)} %param.16) | copy-start | bytes 6291460
  32.0 4.6 %copy-start.9 = (s32[1024,8]{0,1:T(8,128)S(1)}, s32[1024,8]{0,1:T(8,128)}, u32[]{:S(2)}) copy-start(s32[1024,8]{0,1:T(8,128)} %param.21) | copy-start | bytes 98308
  32.0 23.8 %all-to-all-start.1 = ((bf16[128,16,256]{2,1,0:T(8,128)(2,1)}), bf16[128,16,256]{2,1,0:T(8,128)(2,1)S(1)}, u32[]{:S(2)}, u32[]{:S(2)}) async-start(bf16[128,16,256]{2,1,0:T(8,128)(2,1)} %bitcast.51), calls=%async_computation.1 | async-start | bytes 2097152 | tf_op jit(solution)/shard_map/all_to_all | solution.py:658
  36.7 4.5 %copy-start.10 = (s32[1024,8]{0,1:T(8,128)S(1)}, s32[1024,8]{0,1:T(8,128)}, u32[]{:S(2)}) copy-start(s32[1024,8]{0,1:T(8,128)} %param.22) | copy-start | bytes 98308
  41.2 14.7 %copy-start.5 = (s32[1024]{0:T(1024)S(1)}, s32[1024]{0:T(1024)}, u32[]{:S(2)}) copy-start(s32[1024]{0:T(1024)} %param.20) | copy-start | bytes 12292
  59.1 13.0 %collective-permute-start = (bf16[64,1024]{1,0:T(8,128)(2,1)S(1)}, bf16[64,1024]{1,0:T(8,128)(2,1)S(1)}, u32[]{:S(2)}, u32[]{:S(2)}) collective-permute-start(bf16[64,1024]{1,0:T(8,128)(2,1)S(1)} %get-tuple-element.47), channel_id=1, source_target_pairs={{1,0},{2,1},{3,2},{4,3},{5,4},{6,5},{7,6},{8,7},{9,8},{10,9},{11,1... | collective-permute-start | bytes 393224 | tf_op jit(solution)/shard_map/ppermute | solution.py:699
  60.1 11.9 %collective-permute-start.1 = (bf16[64,1024]{1,0:T(8,128)(2,1)S(1)}, bf16[64,1024]{1,0:T(8,128)(2,1)S(1)}, u32[]{:S(2)}, u32[]{:S(2)}) collective-permute-start(bf16[64,1024]{1,0:T(8,128)(2,1)S(1)} %get-tuple-element.48), channel_id=1, source_target_pairs={{0,1},{1,2},{2,3},{3,4},{4,5},{5,6},{6,7},{7,8},{8,9},{9,10},{10,1... | collective-permute-start | bytes 393224 | tf_op jit(solution)/shard_map/ppermute | solution.py:698
  67.3 2.3 %copy-start.16 = (bf16[1024,1024]{1,0:T(8,128)(2,1)S(1)}, bf16[1024,1024]{1,0:T(8,128)(2,1)}, u32[]{:S(2)}) copy-start(bf16[1024,1024]{1,0:T(8,128)(2,1)} %get-tuple-element.44) | copy-start | bytes 6291460
  69.7 2.4 %copy-start.1 = (f32[1024,1024]{1,0:T(8,128)S(1)}, f32[1024,1024]{1,0:T(8,128)}, u32[]{:S(2)}) copy-start(f32[1024,1024]{1,0:T(8,128)} %up_ref.1) | copy-start | bytes 12582916
  69.7 2.9 %copy-start.2 = (bf16[1024,1024]{1,0:T(8,128)(2,1)S(1)}, bf16[1024,1024]{1,0:T(8,128)(2,1)}, u32[]{:S(2)}) copy-start(bf16[1024,1024]{1,0:T(8,128)(2,1)} %wn_ref.6) | copy-start | bytes 6291460
  69.7 2.9 %copy-start.3 = (bf16[128,1024]{1,0:T(8,128)(2,1)S(1)}, bf16[128,1024]{1,0:T(8,128)(2,1)}, u32[]{:S(2)}) copy-start(bf16[128,1024]{1,0:T(8,128)(2,1)} %get-tuple-element.46.edge_t_ref) | copy-start | bytes 786436
  69.7 2.9 %copy-start.4 = (bf16[1024,128]{1,0:T(8,128)(2,1)S(1)}, bf16[1024,128]{1,0:T(8,128)(2,1)}, u32[]{:S(2)}) copy-start(bf16[1024,128]{1,0:T(8,128)(2,1)} %get-tuple-element.45.edge_ref) | copy-start | bytes 786436
  81.5 2.5 %copy-start.8 = (bf16[1024,1024]{1,0:T(8,128)(2,1)}, bf16[1024,1024]{1,0:T(8,128)(2,1)S(1)}, u32[]{:S(2)}) copy-start(bf16[1024,1024]{1,0:T(8,128)(2,1)S(1)} %get-tuple-element.51) | copy-start | bytes 6291460
  81.5 4.5 %copy-start.6 = (bf16[1024,1024]{1,0:T(8,128)(2,1)}, bf16[1024,1024]{1,0:T(8,128)(2,1)S(1)}, u32[]{:S(2)}) copy-start(bf16[1024,1024]{1,0:T(8,128)(2,1)S(1)} %get-tuple-element.50) | copy-start | bytes 6291460
  84.0 4.4 %collective-permute-start.5 = (bf16[1024,1024]{1,0:T(8,128)(2,1)S(1)}, bf16[1024,1024]{1,0:T(8,128)(2,1)S(1)}, u32[]{:S(2)}, u32[]{:S(2)}) collective-permute-start(bf16[1024,1024]{1,0:T(8,128)(2,1)S(1)} %fusion.7), channel_id=1, source_target_pairs={{0,1},{1,0},{2,3},{3,2},{4,5},{5,4},{6,7},{7,6},{8,9},{9,8},{10,11... | collective-permute-start | bytes 6291464 | tf_op jit(solution)/shard_map/ppermute | solution.py:668
  84.1 27.5 %collective-permute-start.3 = (f32[64,1024]{1,0:T(8,128)S(1)}, f32[64,1024]{1,0:T(8,128)S(1)}, u32[]{:S(2)}, u32[]{:S(2)}) collective-permute-start(f32[64,1024]{1,0:T(8,128)S(1)} %get-tuple-element.71), channel_id=1, source_target_pairs={{1,0},{2,1},{3,2},{4,3},{5,4},{6,5},{7,6},{8,7},{9,8},{10,9},{11,1... | collective-permute-start | bytes 786440 | tf_op jit(solution)/shard_map/ppermute | solution.py:707
  84.7 26.9 %collective-permute-start.2 = (f32[64,1024]{1,0:T(8,128)S(1)}, f32[64,1024]{1,0:T(8,128)S(1)}, u32[]{:S(2)}, u32[]{:S(2)}) collective-permute-start(f32[64,1024]{1,0:T(8,128)S(1)} %get-tuple-element.72), channel_id=1, source_target_pairs={{0,1},{1,2},{2,3},{3,4},{4,5},{5,6},{6,7},{7,8},{8,9},{9,10},{10,1... | collective-permute-start | bytes 786440 | tf_op jit(solution)/shard_map/ppermute | solution.py:706
  90.6 44.0 %all-to-all-start.3 = ((bf16[128,8,1024]{2,1,0:T(8,128)(2,1)}), bf16[128,8,1024]{2,1,0:T(8,128)(2,1)}, u32[]{:S(2)}, u32[]{:S(2)}) async-start(bf16[128,8,1024]{2,1,0:T(8,128)(2,1)} %fusion), calls=%async_computation.3 | async-start | bytes 4194304 | tf_op jit(solution)/shard_map/all_to_all | solution.py:658
  104.5 4.7 %copy-start.7 = (bf16[1024,1024]{1,0:T(8,128)(2,1)S(1)}, bf16[1024,1024]{1,0:T(8,128)(2,1)}, u32[]{:S(2)}) copy-start(bf16[1024,1024]{1,0:T(8,128)(2,1)} %copy-done.6) | copy-start | bytes 6291460
  111.6 9.7 %copy-start.13 = (bf16[1024,256]{1,0:T(8,128)(2,1)S(1)}, bf16[1024,256]{1,0:T(8,128)(2,1)}, u32[]{:S(2)}) copy-start(bf16[1024,256]{1,0:T(8,128)(2,1)} %get-tuple-element.57) | copy-start | bytes 1572868
  111.6 9.7 %copy-start.14 = (bf16[1024,256]{1,0:T(8,128)(2,1)S(1)}, bf16[1024,256]{1,0:T(8,128)(2,1)}, u32[]{:S(2)}) copy-start(bf16[1024,256]{1,0:T(8,128)(2,1)} %get-tuple-element.58) | copy-start | bytes 1572868
  121.3 3.7 %copy-start.12 = (bf16[1024,1024]{1,0:T(8,128)(2,1)S(1)}, bf16[1024,1024]{1,0:T(8,128)(2,1)}, u32[]{:S(2)}) copy-start(bf16[1024,1024]{1,0:T(8,128)(2,1)} %get-tuple-element.59) | copy-start | bytes 6291460
  123.8 2.8 %collective-permute-start.4 = (bf16[256,1024]{1,0:T(8,128)(2,1)S(1)}, bf16[256,1024]{1,0:T(8,128)(2,1)S(1)}, u32[]{:S(2)}, u32[]{:S(2)}) collective-permute-start(bf16[256,1024]{1,0:T(8,128)(2,1)S(1)} %convolution_convert_fusion), channel_id=1, source_target_pairs={{0,1},{1,0},{2,3},{3,2},{4,5},{5,4},{6,7},{7,6},{8,9},{9,8},{10,11... | collective-permute-start | bytes 1572872 | tf_op jit(solution)/shard_map/ppermute | solution.py:668
  125.7 1.2 copy-start.15
  134.6 30.1 %all-to-all-start.2 = ((bf16[128,24,256]{2,1,0:T(8,128)(2,1)}), bf16[128,24,256]{2,1,0:T(8,128)(2,1)}, u32[]{:S(2)}, u32[]{:S(2)}) async-start(bf16[128,24,256]{2,1,0:T(8,128)(2,1)} %pad_maximum_fusion), calls=%async_computation.2 | async-start | bytes 3145728 | tf_op jit(solution)/shard_map/all_to_all | solution.py:658
  166.6 44.1 %copy-start.11 = (f32[4096]{0:T(1024)S(1)}, f32[4096]{0:T(1024)}, u32[]{:S(2)}) copy-start(f32[4096]{0:T(1024)} %param.13) | copy-start | bytes 49156
  208.3 16.4 %collective-permute-start.6 = (bf16[128,8,1280]{2,1,0:T(8,128)(2,1)}, bf16[128,8,1280]{2,1,0:T(8,128)(2,1)}, u32[]{:S(2)}, u32[]{:S(2)}) collective-permute-start(bf16[128,8,1280]{2,1,0:T(8,128)(2,1)} %all_to_all.32.mine_ref), channel_id=1, source_target_pairs={{0,1},{1,0},{2,3},{3,2},{4,5},{5,4},{6,7},{7,6},{8,9},{9,8},{10,11... | collective-permute-start | bytes 7864328 | tf_op jit(solution)/shard_map/ppermute | solution.py:725

commit v2 on v1

--- a/solution.py
+++ b/solution.py
@@ -154,17 +154,18 @@
     )(nbr_t)
 
 
-def pick_kernel(inc_ref, table_ref, out_ref, col_ref, acc_ref, turn_ref):
+def pick_kernel(inc_ref, table_ref, out_ref, col_ref, acc_ref, wide_ref):
     i = pl.program_id(0)
     peers, cap = inc_ref.shape
-    rows, width = table_ref.shape
+    rows, _ = table_ref.shape
 
     @pl.when(i == 0)
     def _():
         for c in range(cap):
-            col_ref[c * peers : (c + 1) * peers, :] = jnp.broadcast_to(
+            wide_ref[pl.ds(c, peers, stride=cap), :] = jnp.broadcast_to(
                 inc_ref[:, c : c + 1], (peers, 128)
-            ).astype(I16)
+            )
+        col_ref[...] = wide_ref[...].astype(I16)
         acc_ref[...] = jnp.zeros(acc_ref.shape, F32)
 
     chunk = table_ref[...].astype(BF)
@@ -176,13 +177,7 @@
 
     @pl.when(i == pl.num_programs(0) - 1)
     def _():
-        for c in range(cap):
-            for h in range(width // 128):
-                turn_ref.at[h][pl.ds(c, peers, stride=cap), :] = acc_ref[
-                    c * peers : (c + 1) * peers, h * 128 : (h + 1) * 128
-                ]
-        for h in range(width // 128):
-            out_ref[:, h * 128 : (h + 1) * 128] = turn_ref[h].astype(BF)
+        out_ref[...] = acc_ref[...].astype(BF)
 
 
 def pick(incoming, table):
@@ -202,7 +197,7 @@
         scratch_shapes=[
             pltpu.VMEM((slots, 128), I16),
             pltpu.VMEM((slots, width), F32),
-            pltpu.VMEM((width // 128, slots, 128), F32),
+            pltpu.VMEM((slots, 128), I32),
         ],
         compiler_params=params(24, "arbitrary"),
         name="pick",
@@ -280,7 +275,7 @@
 def layer_one(slot, fetched, adj, w_self, w_nbr):
     nodes, fetch = adj.shape
     emb, hid = w_self.shape
-    block = 256
+    block = 512
     rows = lambda i: (i, 0)
     whole = lambda i: (0, 0)
     return pl.pallas_call(
@@ -305,7 +300,7 @@
             pltpu.HBM((nodes, hid), F32),
             jax.ShapeDtypeStruct((nodes, hid), BF),
         ),
-        compiler_params=params(20, "arbitrary"),
+        compiler_params=params(28, "arbitrary"),
         cost_estimate=cost(2 << 30),
         name="layer_one",
     )(slot, fetched, in_hbm(adj), in_hbm(w_self), in_hbm(w_nbr))
@@ -575,12 +570,12 @@
     rows, width = rest.shape[1:]
     return pl.pallas_call(
         spread_one_kernel,
-        grid=(1,),
+        grid=(lanes // 128,),
         in_specs=[
-            pl.BlockSpec((peers, rows, lanes), lambda i: (0, held // rows - 1, 0)),
+            pl.BlockSpec((peers, rows, 128), lambda i: (0, held // rows - 1, i)),
             pl.BlockSpec(memory_space=pl.ANY),
         ],
-        out_specs=pl.BlockSpec((peers, rows, lanes), lambda i: (0, 0, width // lanes - 1)),
+        out_specs=pl.BlockSpec((peers, rows, 128), lambda i: (0, 0, (width - lanes) // 128 + i)),
         out_shape=pltpu.HBM(rest.shape, BF),
         input_output_aliases={1: 0},
         compiler_params=params(8, "arbitrary"),

time: 229 us -> 227 us (level)
  no operation moved by 1% of the time
where the time goes in v2:
time: 227 us; the launch traced here: 226 us
  Pallas kernels  68.5 us (30%)
  blocking collectives  62.5 us (28%)
  waiting for transfers between devices  38.2 us (17%)
  starting transfers between devices  29.9 us (13%)
  matrix products  19.9 us (9%)
  other arithmetic  4.34 us (2%)
    all_to_all x2, blocking collectives, exchange(): return lax.all_to_all(x, AXES, 0, 0, tiled=True)  62.5 us
    all_to_all x3, waiting for transfers between devices, exchange(): return lax.all_to_all(x, AXES, 0, 0, tiled=True)  37.4 us
    all_to_all x3, starting transfers between devices, exchange(): return lax.all_to_all(x, AXES, 0, 0, tiled=True)  23.9 us
    pallas_call x1, Pallas kernels, update(): pl.pallas_call(update_kernel, grid=(rows // block,), in_specs=[pl.BlockSp...  11.3 us
    pallas_call x1, Pallas kernels, back_one(): pl.pallas_call(back_one_kernel, grid=(nodes // block,), in_specs=[pl.Bloc...  9.66 us
    dot_general x3, matrix products, nn(): lax.dot_general(a, b, (((1,), (0,)), ((), ())), preferred_element_type=F32)  9.35 us
    pallas_call x2, Pallas kernels, counts(): pl.pallas_call(lambda *refs: counts_kernel(shift, sum(widths), *refs), gr...  9.18 us
    pallas_call x1, Pallas kernels, layer_two(): pl.pallas_call(layer_two_kernel, grid=(nodes // block,), in_specs=[pl.Blo...  8.92 us
  transfers between devices with their start and end apart: 10, of which 4 were waited for; matrix products, arithmetic and copies ran while one was open for 10% of the time, Pallas kernels for 19%

profile of v2, /device:TPU:1, one launch (start us, length us, event | category | flops | bytes accessed | tf_op | source)
XLA Modules:
  0.0 226.0 jit_solution(13556502057011035591)
XLA Ops:
  0.6 0.0 copy-start
  0.6 1.5 prep.1
  2.2 20.8 %all_to_all.31 = s32[128,1,16]{2,1,0:T(1,128)S(1)} all-to-all(s32[128,1,16]{2,1,0:T(1,128)S(1)} %bitcast.44), channel_id=1, replica_groups=mesh['grp'=4,'dom'=32] {'grp','dom'}, dimensions={0} | all-to-all | bytes 16384 | tf_op jit(solution)/shard_map/all_to_all | solution.py:653
  23.0 8.1 %pick.1 = bf16[2048,256]{1,0:T(8,128)(2,1)} custom-call(s32[128,16]{1,0:T(8,128)S(1)} %bitcast.43, f32[4096,256]{1,0:T(8,128)} %table_ref.3), custom_call_target="tpu_custom_call" | custom-call | tf_op jit(solution)/shard_map/pick/pallas_call | solution.py:188
  31.1 4.6 %all-to-all-start.1 = ((bf16[128,16,256]{2,1,0:T(8,128)(2,1)}), bf16[128,16,256]{2,1,0:T(8,128)(2,1)S(1)}, u32[]{:S(2)}, u32[]{:S(2)}) async-start(bf16[128,16,256]{2,1,0:T(8,128)(2,1)} %bitcast.51), calls=%async_computation.1 | async-start | bytes 2097152 | tf_op jit(solution)/shard_map/all_to_all | solution.py:653
  35.8 4.5 %shard_map.171 = (bf16[1024,1024]{1,0:T(8,128)(2,1)}, bf16[1024,1024]{1,0:T(8,128)(2,1)}) custom-call(s32[8,1024]{1,0:T(8,128)S(1)} %bitcast.48), custom_call_target="tpu_custom_call" | custom-call | flops 4294967296 | bytes 4194304 | tf_op jit(solution)/shard_map/pallas_call | solution.py:146
  40.3 4.7 %shard_map.172 = (bf16[1024,1024]{1,0:T(8,128)(2,1)}, bf16[1024,1024]{1,0:T(8,128)(2,1)}, bf16[128,1024]{1,0:T(8,128)(2,1)}, bf16[1024,128]{1,0:T(8,128)(2,1)}) custom-call(s32[8,1024]{1,0:T(8,128)S(1)} %bitcast.49), custom_call_target="tpu_custom_call" | custom-call | flops 4294967296 | bytes 4194304 | tf_op jit(solution)/shard_map/pallas_call | solution.py:146
  44.9 10.0 %all-to-all-done.1 = bf16[128,16,256]{2,1,0:T(8,128)(2,1)S(1)} async-done(((bf16[128,16,256]{2,1,0:T(8,128)(2,1)}), bf16[128,16,256]{2,1,0:T(8,128)(2,1)S(1)}, u32[]{:S(2)}, u32[]{:S(2)}) %all-to-all-start.1) | async-done | bytes 1048608 | tf_op jit(solution)/shard_map/all_to_all | solution.py:653
  55.0 3.2 %border.1 = (bf16[1024,256]{1,0:T(8,128)(2,1)S(1)}, bf16[64,1024]{1,0:T(8,128)(2,1)S(1)}, bf16[64,1024]{1,0:T(8,128)(2,1)S(1)}) custom-call(s32[1,1024]{1,0:T(1,128)S(1)} %get-tuple-element.39.pos_ref, s32[1,1024]{1,0:T(1,128)S(1)} %bitcast.45, bf16[2048,256]{1,0:T(8,128)(2,1)S(1)} %bitcast.42, ...), custom_call_target="tpu_custom_call" | custom-call | tf_op jit(solution)/shard_map/border/pallas_call | solution.py:236
  58.2 1.0 collective-permute-start
  59.2 0.8 collective-permute-start.1
  60.0 5.8 %layer_one.1 = (bf16[1024,256]{1,0:T(8,128)(2,1)}, bf16[1024,256]{1,0:T(8,128)(2,1)}, f32[1024,1024]{1,0:T(8,128)}, bf16[1024,1024]{1,0:T(8,128)(2,1)S(1)}) custom-call(s32[1,1024]{1,0:T(1,128)S(1)} %bitcast.46, bf16[1024,256]{1,0:T(8,128)(2,1)S(1)} %get-tuple-element.42.fetched_ref, bf16[1024,1024]{1,0:T(8,128)(2,1)} %get-tuple-element.41.head_ref.tail_ref.adj_ref, ...), custom_call_target="tpu_custom_call" | custom-call | flops 2147483648 | bytes 4194304 | tf_op jit(solution)/shard_map/layer_one/pallas_call | solution.py:281
  65.8 2.3 %fusion.16.own_ref = f32[1024,1024]{1,0:T(8,128)S(1)} fusion(bf16[1024,1024]{1,0:T(8,128)(2,1)S(1)} %get-tuple-element.43, bf16[1024,1024]{1,0:T(8,128)(2,1)S(1)} %copy-done), kind=kOutput, calls=%fused_computation.20 | convolution fusion | flops 2147483648 | bytes 8388608 | tf_op jit(solution)/shard_map/dot_general | solution.py:25
  68.2 2.3 %convolution_bitcast_fusion.pool_ref = f32[1024,1024]{1,0:T(8,128)S(1)} fusion(bf16[1024,1024]{1,0:T(8,128)(2,1)S(1)} %copy-done.16, bf16[1024,1024]{1,0:T(8,128)(2,1)S(1)} %get-tuple-element.43), kind=kOutput, calls=%fused_computation.2 | convolution fusion | flops 2147483648 | bytes 8388608 | tf_op jit(solution)/shard_map/dot_general | solution.py:25
  70.6 0.5 copy-done.2
  71.0 0.0 copy-done.4
  71.1 8.9 %layer_two.1 = (bf16[1024,1024]{1,0:T(8,128)(2,1)}, bf16[1024,1024]{1,0:T(8,128)(2,1)S(1)}, bf16[1024,1024]{1,0:T(8,128)(2,1)S(1)}, bf16[1024,1024]{1,0:T(8,128)(2,1)S(1)}, f32[128,1024]{1,0:T(8,128)S(1)}) custom-call(f32[1024,1024]{1,0:T(8,128)S(1)} %fusion.16.own_ref, f32[1024,1024]{1,0:T(8,128)S(1)} %convolution_bitcast_fusion.pool_ref, ...), custom_call_target="tpu_custom_call" | custom-call | tf_op jit(solution)/shard_map/layer_two/pallas_call | solution.py:345
  80.0 2.5 %fusion.7 = bf16[1024,1024]{1,0:T(8,128)(2,1)S(1)} fusion(bf16[1024,1024]{1,0:T(8,128)(2,1)S(1)} %get-tuple-element.50, bf16[1024,1024]{1,0:T(8,128)(2,1)S(1)} %get-tuple-element.62, bf16[1024,1024]{1,0:T(8,128)(2,1)S(1)} %get-tuple-element.43, pred[]{:T(512)S(6)} %eq.8), kind=kOutput, calls=%fused_computation.10 | convolution fusion | flops 2149580800 | bytes 8388609 | tf_op jit(solution)/shard_map/dot_general | solution.py:33
  82.5 0.1 collective-permute-start.5
  82.6 0.6 collective-permute-start.3
  83.2 1.3 collective-permute-start.2
  84.4 2.5 %fusion.3 = f32[1024,1024]{1,0:T(8,128)S(1)} fusion(bf16[1024,1024]{1,0:T(8,128)(2,1)S(1)} %get-tuple-element.50, bf16[1024,1024]{1,0:T(8,128)(2,1)S(1)} %get-tuple-element.43, bf16[1024,1024]{1,0:T(8,128)(2,1)S(1)} %get-tuple-element.62, pred[]{:T(512)S(6)} %eq.8), kind=kOutput, calls=%fused_computation.6 | convolution fusion | flops 2148532224 | bytes 10485761 | tf_op jit(solution)/shard_map/dot_general | solution.py:33
  86.9 2.2 fusion
  89.1 13.9 %all-to-all-start.3 = ((bf16[128,8,1024]{2,1,0:T(8,128)(2,1)}), bf16[128,8,1024]{2,1,0:T(8,128)(2,1)}, u32[]{:S(2)}, u32[]{:S(2)}) async-start(bf16[128,8,1024]{2,1,0:T(8,128)(2,1)} %fusion), calls=%async_computation.3 | async-start | bytes 4194304 | tf_op jit(solution)/shard_map/all_to_all | solution.py:653
  103.0 4.7 %fusion.17 = f32[1024,1024]{0,1:T(8,128)S(1)} fusion(bf16[1024,1024]{1,0:T(8,128)(2,1)} %get-tuple-element.52, bf16[1024,1024]{1,0:T(8,128)(2,1)} %copy-done.8), kind=kOutput, calls=%fused_computation.21 | convolution fusion | flops 2147483648 | bytes 8388608 | tf_op jit(solution)/shard_map/dot_general | solution.py:25
  107.7 2.4 %bitcast_add_fusion.gh_ref = f32[1024,1024]{1,0:T(8,128)S(1)} fusion(f32[1024,1024]{0,1:T(8,128)S(1)} %fusion.17, bf16[1024,1024]{1,0:T(8,128)(2,1)S(1)} %copy-done.7, bf16[1024,1024]{1,0:T(8,128)(2,1)S(1)} %copy-done), kind=kOutput, calls=%fused_computation | convolution fusion | flops 2148532224 | bytes 12582912 | tf_op jit(solution)/shard_map/dot_general | solution.py:29
  110.1 9.7 %back_one.1 = (bf16[1024,1024]{1,0:T(8,128)(2,1)}, bf16[2048,256]{1,0:T(8,128)(2,1)}) custom-call(f32[1024,1024]{1,0:T(8,128)S(1)} %bitcast_add_fusion.gh_ref, f32[64,1024]{1,0:T(8,128)S(1)} %collective-permute-done.2.first_ref, f32[64,1024]{1,0:T(8,128)S(1)} %collective-permute-done.3.last_ref, f32[1024,1024]{1,0:T(8,128)} %get-tuple-element.54.before_ref, ...), custom_call_target="tpu_custom_call" | custom-call | tf_op jit(solution)/shard_map/back_one/pallas_call | solution.py:425
  119.8 2.5 %convolution_convert_fusion = bf16[256,1024]{1,0:T(8,128)(2,1)S(1)} fusion(bf16[1024,1024]{1,0:T(8,128)(2,1)} %get-tuple-element.59, bf16[1024,256]{1,0:T(8,128)(2,1)S(1)} %copy-done.14, bf16[1024,256]{1,0:T(8,128)(2,1)S(1)} %copy-done.13, pred[]{:T(512)S(6)} %eq.8), kind=kOutput, calls=%fused_computation.12 | convolution fusion | flops 537395200 | bytes 3670017 | tf_op jit(solution)/shard_map/dot_general | solution.py:33
  122.3 1.2 collective-permute-start.4
  123.5 0.7 fusion.11
  124.3 0.8 collective-permute-done.4
  125.0 0.1 add_convert_fusion.1
  125.2 0.2 copy-done.15
  125.5 1.2 pad_maximum_fusion
  126.7 6.4 %all-to-all-done.3.parts_ref = bf16[128,8,1024]{2,1,0:T(8,128)(2,1)} async-done(((bf16[128,8,1024]{2,1,0:T(8,128)(2,1)}), bf16[128,8,1024]{2,1,0:T(8,128)(2,1)}, u32[]{:S(2)}, u32[]{:S(2)}) %all-to-all-start.3) | async-done | bytes 2097184 | tf_op jit(solution)/shard_map/all_to_all | solution.py:653
  133.1 5.4 %all-to-all-start.2 = ((bf16[128,24,256]{2,1,0:T(8,128)(2,1)}), bf16[128,24,256]{2,1,0:T(8,128)(2,1)}, u32[]{:S(2)}, u32[]{:S(2)}) async-start(bf16[128,24,256]{2,1,0:T(8,128)(2,1)} %pad_maximum_fusion), calls=%async_computation.2 | async-start | bytes 3145728 | tf_op jit(solution)/shard_map/all_to_all | solution.py:653
  138.5 1.7 two_sum.1.two_ref
  140.3 1.9 spread_two.1.rest_ref
  142.1 21.1 %all-to-all-done.2.got_ref = bf16[128,24,256]{2,1,0:T(8,128)(2,1)} async-done(((bf16[128,24,256]{2,1,0:T(8,128)(2,1)}), bf16[128,24,256]{2,1,0:T(8,128)(2,1)}, u32[]{:S(2)}, u32[]{:S(2)}) %all-to-all-start.2) | async-done | bytes 1572896 | tf_op jit(solution)/shard_map/all_to_all | solution.py:653
  163.2 1.9 spread_one.1
  165.1 41.6 %all_to_all.32.mine_ref = bf16[128,8,1280]{2,1,0:T(8,128)(2,1)} all-to-all(bf16[128,8,1280]{2,1,0:T(8,128)(2,1)} %spread_one.1), channel_id=1, replica_groups=mesh['grp'=4,'dom'=32] {'grp','dom'}, dimensions={0} | all-to-all | bytes 5242880 | tf_op jit(solution)/shard_map/all_to_all | solution.py:653
  206.7 1.0 collective-permute-start.6
  207.7 0.5 broadcast.4
  208.2 0.8 reduce.3
  209.0 0.1 reshape.76.inc_ref
  209.2 11.3 %update.1 = (f32[4096,256]{1,0:T(8,128)}, f32[8,1,512]{2,1,0:T(1,128)}) custom-call(s32[1,2048]{1,0:T(1,128)S(1)} %reshape.76.inc_ref, bf16[128,24,256]{2,1,0:T(8,128)(2,1)} %all-to-all-done.2.got_ref, f32[4096,256]{1,0:T(8,128)} %table_ref.3, f32[8,1,512]{2,1,0:T(1,128)S(1)} %bitcast.50), custom_call_target="tpu_custom_call" | custom-call | flops 4294967296 | bytes 4194304 | tf_op jit(solution)/shard_map/update/pallas_call | solution.py:489
  220.5 2.7 %shard_map.173 = (bf16[32,8,1024]{2,1,0:T(8,128)(2,1)}, bf16[32,8,1024]{2,1,0:T(8,128)(2,1)}, bf16[128,8,1024]{2,1,0:T(8,128)(2,1)}, bf16[128,8,1024]{2,1,0:T(8,128)(2,1)}) custom-call(s32[1]{0:T(128)} %bitcast.20.which_ref, bf16[128,8,1280]{2,1,0:T(8,128)(2,1)} %all_to_all.32.mine_ref), custom_call_target="tpu_custom_call" | custom-call | tf_op jit(solution)/shard_map/pallas_call | solution.py:637
  223.1 2.7 %shard_map.174 = (bf16[32,8,1024]{2,1,0:T(8,128)(2,1)}, bf16[32,8,1024]{2,1,0:T(8,128)(2,1)}, bf16[128,8,1024]{2,1,0:T(8,128)(2,1)}, bf16[128,8,1024]{2,1,0:T(8,128)(2,1)}) custom-call(s32[1]{0:T(128)} %bitcast.18.which_ref, ...), custom_call_target="tpu_custom_call", output_to_operand_aliasing={{0}: (2, {}), {1}: (3, {}), {2}: (4, {}), {3}: (5, {})} | custom-call | tf_op jit(solution)/shard_map/pallas_call | solution.py:637
  (38 shorter events, 0.2 us)
Async XLA Ops:
  0.6 65.2 %copy-start = (bf16[1024,1024]{1,0:T(8,128)(2,1)S(1)}, bf16[1024,1024]{1,0:T(8,128)(2,1)}, u32[]{:S(2)}) copy-start(bf16[1024,1024]{1,0:T(8,128)(2,1)} %param.16) | copy-start | bytes 6291460
  31.1 4.6 %copy-start.9 = (s32[1024,8]{0,1:T(8,128)S(1)}, s32[1024,8]{0,1:T(8,128)}, u32[]{:S(2)}) copy-start(s32[1024,8]{0,1:T(8,128)} %param.21) | copy-start | bytes 98308
  31.1 23.8 %all-to-all-start.1 = ((bf16[128,16,256]{2,1,0:T(8,128)(2,1)}), bf16[128,16,256]{2,1,0:T(8,128)(2,1)S(1)}, u32[]{:S(2)}, u32[]{:S(2)}) async-start(bf16[128,16,256]{2,1,0:T(8,128)(2,1)} %bitcast.51), calls=%async_computation.1 | async-start | bytes 2097152 | tf_op jit(solution)/shard_map/all_to_all | solution.py:653
  35.8 4.5 %copy-start.10 = (s32[1024,8]{0,1:T(8,128)S(1)}, s32[1024,8]{0,1:T(8,128)}, u32[]{:S(2)}) copy-start(s32[1024,8]{0,1:T(8,128)} %param.22) | copy-start | bytes 98308
  40.3 14.7 %copy-start.5 = (s32[1024]{0:T(1024)S(1)}, s32[1024]{0:T(1024)}, u32[]{:S(2)}) copy-start(s32[1024]{0:T(1024)} %param.20) | copy-start | bytes 12292
  58.2 12.4 %collective-permute-start = (bf16[64,1024]{1,0:T(8,128)(2,1)S(1)}, bf16[64,1024]{1,0:T(8,128)(2,1)S(1)}, u32[]{:S(2)}, u32[]{:S(2)}) collective-permute-start(bf16[64,1024]{1,0:T(8,128)(2,1)S(1)} %get-tuple-element.47), channel_id=1, source_target_pairs={{1,0},{2,1},{3,2},{4,3},{5,4},{6,5},{7,6},{8,7},{9,8},{10,9},{11,1... | collective-permute-start | bytes 393224 | tf_op jit(solution)/shard_map/ppermute | solution.py:694
  59.2 11.4 %collective-permute-start.1 = (bf16[64,1024]{1,0:T(8,128)(2,1)S(1)}, bf16[64,1024]{1,0:T(8,128)(2,1)S(1)}, u32[]{:S(2)}, u32[]{:S(2)}) collective-permute-start(bf16[64,1024]{1,0:T(8,128)(2,1)S(1)} %get-tuple-element.48), channel_id=1, source_target_pairs={{0,1},{1,2},{2,3},{3,4},{4,5},{5,6},{6,7},{7,8},{8,9},{9,10},{10,1... | collective-permute-start | bytes 393224 | tf_op jit(solution)/shard_map/ppermute | solution.py:693
  65.8 2.3 %copy-start.16 = (bf16[1024,1024]{1,0:T(8,128)(2,1)S(1)}, bf16[1024,1024]{1,0:T(8,128)(2,1)}, u32[]{:S(2)}) copy-start(bf16[1024,1024]{1,0:T(8,128)(2,1)} %get-tuple-element.44) | copy-start | bytes 6291460
  68.2 2.4 %copy-start.1 = (f32[1024,1024]{1,0:T(8,128)S(1)}, f32[1024,1024]{1,0:T(8,128)}, u32[]{:S(2)}) copy-start(f32[1024,1024]{1,0:T(8,128)} %up_ref.1) | copy-start | bytes 12582916
  68.2 2.9 %copy-start.2 = (bf16[1024,1024]{1,0:T(8,128)(2,1)S(1)}, bf16[1024,1024]{1,0:T(8,128)(2,1)}, u32[]{:S(2)}) copy-start(bf16[1024,1024]{1,0:T(8,128)(2,1)} %wn_ref.6) | copy-start | bytes 6291460
  68.2 2.9 %copy-start.3 = (bf16[128,1024]{1,0:T(8,128)(2,1)S(1)}, bf16[128,1024]{1,0:T(8,128)(2,1)}, u32[]{:S(2)}) copy-start(bf16[128,1024]{1,0:T(8,128)(2,1)} %get-tuple-element.46.edge_t_ref) | copy-start | bytes 786436
  68.2 2.9 %copy-start.4 = (bf16[1024,128]{1,0:T(8,128)(2,1)S(1)}, bf16[1024,128]{1,0:T(8,128)(2,1)}, u32[]{:S(2)}) copy-start(bf16[1024,128]{1,0:T(8,128)(2,1)} %get-tuple-element.45.edge_ref) | copy-start | bytes 786436
  80.0 2.5 %copy-start.8 = (bf16[1024,1024]{1,0:T(8,128)(2,1)}, bf16[1024,1024]{1,0:T(8,128)(2,1)S(1)}, u32[]{:S(2)}) copy-start(bf16[1024,1024]{1,0:T(8,128)(2,1)S(1)} %get-tuple-element.51) | copy-start | bytes 6291460
  80.0 4.5 %copy-start.6 = (bf16[1024,1024]{1,0:T(8,128)(2,1)}, bf16[1024,1024]{1,0:T(8,128)(2,1)S(1)}, u32[]{:S(2)}) copy-start(bf16[1024,1024]{1,0:T(8,128)(2,1)S(1)} %get-tuple-element.50) | copy-start | bytes 6291460
  82.5 4.4 %collective-permute-start.5 = (bf16[1024,1024]{1,0:T(8,128)(2,1)S(1)}, bf16[1024,1024]{1,0:T(8,128)(2,1)S(1)}, u32[]{:S(2)}, u32[]{:S(2)}) collective-permute-start(bf16[1024,1024]{1,0:T(8,128)(2,1)S(1)} %fusion.7), channel_id=1, source_target_pairs={{0,1},{1,0},{2,3},{3,2},{4,5},{5,4},{6,7},{7,6},{8,9},{9,8},{10,11... | collective-permute-start | bytes 6291464 | tf_op jit(solution)/shard_map/ppermute | solution.py:663
  82.6 27.5 %collective-permute-start.3 = (f32[64,1024]{1,0:T(8,128)S(1)}, f32[64,1024]{1,0:T(8,128)S(1)}, u32[]{:S(2)}, u32[]{:S(2)}) collective-permute-start(f32[64,1024]{1,0:T(8,128)S(1)} %get-tuple-element.71), channel_id=1, source_target_pairs={{1,0},{2,1},{3,2},{4,3},{5,4},{6,5},{7,6},{8,7},{9,8},{10,9},{11,1... | collective-permute-start | bytes 786440 | tf_op jit(solution)/shard_map/ppermute | solution.py:702
  83.2 26.9 %collective-permute-start.2 = (f32[64,1024]{1,0:T(8,128)S(1)}, f32[64,1024]{1,0:T(8,128)S(1)}, u32[]{:S(2)}, u32[]{:S(2)}) collective-permute-start(f32[64,1024]{1,0:T(8,128)S(1)} %get-tuple-element.72), channel_id=1, source_target_pairs={{0,1},{1,2},{2,3},{3,4},{4,5},{5,6},{6,7},{7,8},{8,9},{9,10},{10,1... | collective-permute-start | bytes 786440 | tf_op jit(solution)/shard_map/ppermute | solution.py:701
  89.1 44.0 %all-to-all-start.3 = ((bf16[128,8,1024]{2,1,0:T(8,128)(2,1)}), bf16[128,8,1024]{2,1,0:T(8,128)(2,1)}, u32[]{:S(2)}, u32[]{:S(2)}) async-start(bf16[128,8,1024]{2,1,0:T(8,128)(2,1)} %fusion), calls=%async_computation.3 | async-start | bytes 4194304 | tf_op jit(solution)/shard_map/all_to_all | solution.py:653
  103.0 4.7 %copy-start.7 = (bf16[1024,1024]{1,0:T(8,128)(2,1)S(1)}, bf16[1024,1024]{1,0:T(8,128)(2,1)}, u32[]{:S(2)}) copy-start(bf16[1024,1024]{1,0:T(8,128)(2,1)} %copy-done.6) | copy-start | bytes 6291460
  110.1 9.7 %copy-start.13 = (bf16[1024,256]{1,0:T(8,128)(2,1)S(1)}, bf16[1024,256]{1,0:T(8,128)(2,1)}, u32[]{:S(2)}) copy-start(bf16[1024,256]{1,0:T(8,128)(2,1)} %get-tuple-element.57) | copy-start | bytes 1572868
  110.1 9.7 %copy-start.14 = (bf16[1024,256]{1,0:T(8,128)(2,1)S(1)}, bf16[1024,256]{1,0:T(8,128)(2,1)}, u32[]{:S(2)}) copy-start(bf16[1024,256]{1,0:T(8,128)(2,1)} %get-tuple-element.58) | copy-start | bytes 1572868
  119.8 3.7 %copy-start.12 = (bf16[1024,1024]{1,0:T(8,128)(2,1)S(1)}, bf16[1024,1024]{1,0:T(8,128)(2,1)}, u32[]{:S(2)}) copy-start(bf16[1024,1024]{1,0:T(8,128)(2,1)} %get-tuple-element.59) | copy-start | bytes 6291460
  122.3 2.8 %collective-permute-start.4 = (bf16[256,1024]{1,0:T(8,128)(2,1)S(1)}, bf16[256,1024]{1,0:T(8,128)(2,1)S(1)}, u32[]{:S(2)}, u32[]{:S(2)}) collective-permute-start(bf16[256,1024]{1,0:T(8,128)(2,1)S(1)} %convolution_convert_fusion), channel_id=1, source_target_pairs={{0,1},{1,0},{2,3},{3,2},{4,5},{5,4},{6,7},{7,6},{8,9},{9,8},{10,11... | collective-permute-start | bytes 1572872 | tf_op jit(solution)/shard_map/ppermute | solution.py:663
  124.2 1.2 copy-start.15
  133.1 30.1 %all-to-all-start.2 = ((bf16[128,24,256]{2,1,0:T(8,128)(2,1)}), bf16[128,24,256]{2,1,0:T(8,128)(2,1)}, u32[]{:S(2)}, u32[]{:S(2)}) async-start(bf16[128,24,256]{2,1,0:T(8,128)(2,1)} %pad_maximum_fusion), calls=%async_computation.2 | async-start | bytes 3145728 | tf_op jit(solution)/shard_map/all_to_all | solution.py:653
  165.1 44.1 %copy-start.11 = (f32[4096]{0:T(1024)S(1)}, f32[4096]{0:T(1024)}, u32[]{:S(2)}) copy-start(f32[4096]{0:T(1024)} %param.13) | copy-start | bytes 49156
  206.7 16.4 %collective-permute-start.6 = (bf16[128,8,1280]{2,1,0:T(8,128)(2,1)}, bf16[128,8,1280]{2,1,0:T(8,128)(2,1)}, u32[]{:S(2)}, u32[]{:S(2)}) collective-permute-start(bf16[128,8,1280]{2,1,0:T(8,128)(2,1)} %all_to_all.32.mine_ref), channel_id=1, source_target_pairs={{0,1},{1,0},{2,3},{3,2},{4,5},{5,4},{6,7},{7,6},{8,9},{9,8},{10,11... | collective-permute-start | bytes 7864328 | tf_op jit(solution)/shard_map/ppermute | solution.py:720
